TPU v7x, 128 devices: a whole 4x4x4 slice. The times are simulated.
128 devices in a mesh: col: 64 (over y, x, z), grp: 2 (over core).
Axes of the slice: x: 4, y: 4, z: 4, core: 2. Of those that a mesh axis runs over, the one named last changes fastest.
Arguments:
- diag_blocks: float32 [64, 128, 128], P('col'), as said below
- panel_blocks: float32 [64, 2, 128, 128], P('col', 'grp'), as said below
- targets: int32 [64, 2], replicated, may hold values from 0 to 64, as said below
Outputs:
- factor_diag: float32 [64, 128, 128], P('col')
- factor_panel: float32 [64, 2, 128, 128], P('col', 'grp')
Inputs may be any that keep to these rules, and one draw needn't show every extreme that they name: targets[s, 0] is the parent of supernode s and targets[s, 1] = targets[targets[s, 0], 0] its grandparent, 64 where that ancestor lies outside the window; the tree is a binary heap under a random labelling: exactly one root, every supernode has at most two children and at most four grandchildren, and level d holds min(2 ** d, 64 - 2 ** d + 1) supernodes. `diag_blocks`: each block is symmetric positive definite, and every updated diagonal block stays positive definite. `panel_blocks`: every entry lies within 8 / sqrt(128) of zero.
All inputs are finite; a program needn't handle non-finite values.
Results may differ from a plain program's by a relative error of at most 0.00095.
Values may be sent and summed in bfloat16 or wider, within the bound.
A program may use at most 64 MiB of HBM per device.

v0:
```python
import jax
import jax.numpy as jnp
from jax import lax
from jax.sharding import PartitionSpec as P


def picked(x, axis, root):
    return lax.dynamic_index_in_dim(lax.all_gather(x, axis), root, 0, keepdims=False)


def in_order(pieces, dim):
    shape = list(pieces.shape[1:])
    shape[dim] *= pieces.shape[0]
    return jnp.moveaxis(pieces, 0, dim).reshape(shape)


def sent_to_all(x, axis):
    copies = jnp.broadcast_to(x, (lax.axis_size(axis), *x.shape))
    return lax.all_to_all(copies, axis, split_axis=0, concat_axis=0, tiled=True)


def collect(x, axis, dim):
    return in_order(sent_to_all(x, axis), dim)


def from_partner(x, axis, apart):
    return lax.ppermute(x, axis, [(i, i ^ 1 << apart) for i in range(lax.axis_size(axis))])


def node_depth(parent, nodes):
    extended = jnp.concatenate([parent, jnp.array([nodes], jnp.int32)])
    depth = jnp.zeros((nodes,), jnp.int32)
    current = parent
    for index in range(nodes.bit_length()):
        depth = depth + (current < nodes).astype(jnp.int32)
        current = extended[current]
    return depth


def solve_right(lower, panel):

    def one(factor, block):
        return jax.scipy.linalg.solve_triangular(factor, block.T, lower=True).T

    return jax.vmap(one)(lower, panel)


def sibling_rank(target, nodes):
    earlier = jnp.arange(nodes)[None, :] < jnp.arange(nodes)[:, None]
    same = target[:, None] == target[None, :]
    return jnp.sum((same & earlier).astype(jnp.int32), axis=1)


def slot_picker(target, rank, active_nodes, owned_ids, count):
    match = target[None, None, :] == owned_ids[:, None, None]
    match = match & (rank[None, None, :] == jnp.arange(count)[None, :, None])
    match = match & active_nodes[None, None, :]
    return match.astype(jnp.bfloat16)


def select_rows(picker, block_list):
    return jnp.einsum("iqc,cab->iqab", picker, block_list, preferred_element_type=jnp.float32)


def outer_sum(block_list):
    return jnp.einsum("hync,hyxc->hnx", block_list, block_list, preferred_element_type=jnp.float32)


def cross_sum(left_factor, right_factor):
    return jnp.einsum(
        "hync,hyxc->hnx", left_factor, right_factor, preferred_element_type=jnp.float32
    )


def pair_cores(sent):
    return lax.all_gather(sent[:, None], "grp", axis=1, tiled=True)


def spread_nodes(sent, active_nodes, pick_near, pick_far, slots, nodes, present, blanks):
    paired = pair_cores(sent)
    order = jnp.argsort(jnp.where(active_nodes, 0, 1) * nodes + jnp.arange(nodes, dtype=jnp.int32))

    def visit(index, carry):
        node = order[index]
        piece = lax.dynamic_index_in_dim(paired, node % slots, 0, keepdims=False)
        arrived = picked(piece, "col", node // slots).astype(jnp.float32)
        weight_near = lax.dynamic_index_in_dim(pick_near, node, 2, keepdims=False).astype(
            jnp.float32
        )
        weight_far = lax.dynamic_index_in_dim(pick_far, node, 2, keepdims=False).astype(jnp.float32)
        return (
            carry[0] + weight_near[:, :, None, None] * arrived[0][None, None],
            carry[1] + weight_far[:, :, None, None] * arrived[1][None, None],
            carry[2] + weight_near[:, :, None, None] * arrived[1][None, None],
        )

    return lax.fori_loop(0, present, visit, blanks)


def shards(diag_blocks, panel_blocks, targets):
    slots = diag_blocks.shape[0]
    width = diag_blocks.shape[1]
    nodes = targets.shape[0]
    core = lax.axis_index("grp")
    owned_ids = lax.axis_index("col") * slots + jnp.arange(slots, dtype=jnp.int32)
    parent = targets[:, 0]
    grand = targets[:, 1]
    depth = node_depth(parent, nodes)
    rank_near = sibling_rank(parent, nodes)
    rank_far = sibling_rank(grand, nodes)
    owned_tree_depth = jnp.take(depth, owned_ids)
    acc_diag = diag_blocks
    acc_panel = panel_blocks[:, 0]
    out_diag = jnp.zeros_like(diag_blocks)
    output_panel = jnp.zeros_like(acc_panel)
    empty_pair_slots = jnp.zeros((slots, 2, width, width), jnp.float32)
    blank_four = jnp.zeros((slots, 4, width, width), jnp.float32)
    for level in range(nodes.bit_length() - 1, -1, -1):
        wide_mask = (owned_tree_depth == level)[:, None, None]
        lower = jnp.linalg.cholesky(acc_diag)
        solved = solve_right(lower, acc_panel)
        out_diag = jnp.where(wide_mask, lower, out_diag)
        output_panel = jnp.where(wide_mask, solved, output_panel)
        if level == 0:
            break
        sent = jnp.where(wide_mask, solved, 0.0).astype(jnp.bfloat16)
        active_nodes = depth == level
        pick_near = slot_picker(parent, rank_near, active_nodes, owned_ids, 2)
        pick_far = slot_picker(grand, rank_far, active_nodes, owned_ids, 4)
        present = min(2**level, nodes - 2**level + 1)
        crowded = present * 4 > nodes
        if crowded:
            piece = collect(sent, "col", 0)
            near_rows = select_rows(pick_near, piece)
            far_rows = select_rows(pick_far, piece)
            near_rows = near_rows.astype(jnp.bfloat16)
            far_rows = far_rows.astype(jnp.bfloat16)
            own_update = lax.cond(
                core == 0, lambda: outer_sum(near_rows), lambda: outer_sum(far_rows)
            )
            other_update, other_rows = (
                from_partner(own_update.astype(jnp.bfloat16), "grp", 0).astype(own_update.dtype),
                from_partner(near_rows, "grp", 0),
            )
            schur_update = own_update + other_update
            cross = cross_sum(other_rows, near_rows)
        else:
            kids, grandkids, kids_far = spread_nodes(
                sent,
                active_nodes,
                pick_near,
                pick_far,
                slots,
                nodes,
                present,
                (empty_pair_slots, blank_four, empty_pair_slots),
            )
            kids = kids.astype(jnp.bfloat16)
            schur_update = outer_sum(kids) + outer_sum(grandkids.astype(jnp.bfloat16))
            cross = cross_sum(kids_far.astype(jnp.bfloat16), kids)
        acc_diag = acc_diag - schur_update
        acc_panel = acc_panel - jnp.where(core == 0, cross, 0.0)
    return (out_diag, output_panel[:, None])


def solution(mesh):
    placed = (P("col", None, None), P("col", "grp", None, None), P())
    return jax.shard_map(
        shards,
        mesh=mesh,
        in_specs=placed,
        out_specs=(P("col", None, None), P("col", "grp", None, None)),
        check_vma=False,
    )
```

profile of v0, /device:TPU:1, one launch (start us, length us, event | category | flops | bytes accessed | tf_op | source)
XLA Modules:
  0.0 2446.1 jit_solution(8001692143543490750)
XLA Ops:
  15.4 11.7 custom-call.30
  28.4 9.8 custom-call.31
  49.0 65.1 %all-gather.12.cloned.1.call-done = bf16[128,128,128]{2,1,0:T(8,128)(2,1)} async-done(((bf16[2,128,128]{2,1,0:T(8,128)(2,1)}), bf16[128,128,128]{2,1,0:T(8,128)(2,1)}) %all-gather.12.cloned.1.call-update) | async-done | bytes 4194320 | tf_op jit(solution)/shard_map/while/body/eval_jaxpr/all_gather | solution.py:8
  115.7 11.7 custom-call.32
  128.8 9.8 custom-call.33
  147.7 27.1 %all-to-all-done = bf16[64,1,128,128]{3,2,1,0:T(8,128)(2,1)S(1)} async-done(((bf16[64,1,128,128]{3,2,1,0:T(8,128)(2,1)}), bf16[64,1,128,128]{3,2,1,0:T(8,128)(2,1)S(1)}, u32[]{:S(2)}, u32[]{:S(2)}) %all-to-all-start) | async-done | bytes 2097184 | tf_op jit(solution)/shard_map/all_to_all | solution.py:19
  189.6 11.7 custom-call.34
  202.6 9.8 custom-call.35
  215.3 1126.4 %while.88 = (s32[]{:T(128)}, f32[1,2,128,128]{3,2,1,0:T(8,128)S(1)}, f32[1,4,128,128]{3,2,1,0:T(8,128)S(1)}, f32[1,2,128,128]{3,2,1,0:T(8,128)S(1)}, s32[64]{0:T...) while((s32[]{:T(128)}, ...), condition=%wide.region_9.12_spmd.clone, body=%wide.region_8.11_spmd.clone.sunk | while | flops 425996 | bytes 14483734 | solution.py:97
  218.8 63.4 %all-gather.14.cloned.1.call-done = bf16[64,2,128,128]{3,2,1,0:T(8,128)(2,1)} async-done(((bf16[1,2,128,128]{3,2,1,0:T(8,128)(2,1)}), bf16[64,2,128,128]{3,2,1,0:T(8,128)(2,1)}) %all-gather.14.cloned.1.call-update) | async-done | bytes 4194320 | tf_op jit(solution)/shard_map/while/body/eval_jaxpr/all_gather | solution.py:8
  286.8 66.2 %all-gather.14.cloned.1.call-done = bf16[64,2,128,128]{3,2,1,0:T(8,128)(2,1)} async-done(((bf16[1,2,128,128]{3,2,1,0:T(8,128)(2,1)}), bf16[64,2,128,128]{3,2,1,0:T(8,128)(2,1)}) %all-gather.14.cloned.1.call-update) | async-done | bytes 4194320 | tf_op jit(solution)/shard_map/while/body/eval_jaxpr/all_gather | solution.py:8
  357.4 66.0 %all-gather.14.cloned.1.call-done = bf16[64,2,128,128]{3,2,1,0:T(8,128)(2,1)} async-done(((bf16[1,2,128,128]{3,2,1,0:T(8,128)(2,1)}), bf16[64,2,128,128]{3,2,1,0:T(8,128)(2,1)}) %all-gather.14.cloned.1.call-update) | async-done | bytes 4194320 | tf_op jit(solution)/shard_map/while/body/eval_jaxpr/all_gather | solution.py:8
  427.8 66.0 %all-gather.14.cloned.1.call-done = bf16[64,2,128,128]{3,2,1,0:T(8,128)(2,1)} async-done(((bf16[1,2,128,128]{3,2,1,0:T(8,128)(2,1)}), bf16[64,2,128,128]{3,2,1,0:T(8,128)(2,1)}) %all-gather.14.cloned.1.call-update) | async-done | bytes 4194320 | tf_op jit(solution)/shard_map/while/body/eval_jaxpr/all_gather | solution.py:8
  498.3 66.0 %all-gather.14.cloned.1.call-done = bf16[64,2,128,128]{3,2,1,0:T(8,128)(2,1)} async-done(((bf16[1,2,128,128]{3,2,1,0:T(8,128)(2,1)}), bf16[64,2,128,128]{3,2,1,0:T(8,128)(2,1)}) %all-gather.14.cloned.1.call-update) | async-done | bytes 4194320 | tf_op jit(solution)/shard_map/while/body/eval_jaxpr/all_gather | solution.py:8
  568.9 66.2 %all-gather.14.cloned.1.call-done = bf16[64,2,128,128]{3,2,1,0:T(8,128)(2,1)} async-done(((bf16[1,2,128,128]{3,2,1,0:T(8,128)(2,1)}), bf16[64,2,128,128]{3,2,1,0:T(8,128)(2,1)}) %all-gather.14.cloned.1.call-update) | async-done | bytes 4194320 | tf_op jit(solution)/shard_map/while/body/eval_jaxpr/all_gather | solution.py:8
  639.6 66.2 %all-gather.14.cloned.1.call-done = bf16[64,2,128,128]{3,2,1,0:T(8,128)(2,1)} async-done(((bf16[1,2,128,128]{3,2,1,0:T(8,128)(2,1)}), bf16[64,2,128,128]{3,2,1,0:T(8,128)(2,1)}) %all-gather.14.cloned.1.call-update) | async-done | bytes 4194320 | tf_op jit(solution)/shard_map/while/body/eval_jaxpr/all_gather | solution.py:8
  710.4 66.2 %all-gather.14.cloned.1.call-done = bf16[64,2,128,128]{3,2,1,0:T(8,128)(2,1)} async-done(((bf16[1,2,128,128]{3,2,1,0:T(8,128)(2,1)}), bf16[64,2,128,128]{3,2,1,0:T(8,128)(2,1)}) %all-gather.14.cloned.1.call-update) | async-done | bytes 4194320 | tf_op jit(solution)/shard_map/while/body/eval_jaxpr/all_gather | solution.py:8
  781.0 66.0 %all-gather.14.cloned.1.call-done = bf16[64,2,128,128]{3,2,1,0:T(8,128)(2,1)} async-done(((bf16[1,2,128,128]{3,2,1,0:T(8,128)(2,1)}), bf16[64,2,128,128]{3,2,1,0:T(8,128)(2,1)}) %all-gather.14.cloned.1.call-update) | async-done | bytes 4194320 | tf_op jit(solution)/shard_map/while/body/eval_jaxpr/all_gather | solution.py:8
  851.6 66.2 %all-gather.14.cloned.1.call-done = bf16[64,2,128,128]{3,2,1,0:T(8,128)(2,1)} async-done(((bf16[1,2,128,128]{3,2,1,0:T(8,128)(2,1)}), bf16[64,2,128,128]{3,2,1,0:T(8,128)(2,1)}) %all-gather.14.cloned.1.call-update) | async-done | bytes 4194320 | tf_op jit(solution)/shard_map/while/body/eval_jaxpr/all_gather | solution.py:8
  922.1 66.0 %all-gather.14.cloned.1.call-done = bf16[64,2,128,128]{3,2,1,0:T(8,128)(2,1)} async-done(((bf16[1,2,128,128]{3,2,1,0:T(8,128)(2,1)}), bf16[64,2,128,128]{3,2,1,0:T(8,128)(2,1)}) %all-gather.14.cloned.1.call-update) | async-done | bytes 4194320 | tf_op jit(solution)/shard_map/while/body/eval_jaxpr/all_gather | solution.py:8
  992.8 66.2 %all-gather.14.cloned.1.call-done = bf16[64,2,128,128]{3,2,1,0:T(8,128)(2,1)} async-done(((bf16[1,2,128,128]{3,2,1,0:T(8,128)(2,1)}), bf16[64,2,128,128]{3,2,1,0:T(8,128)(2,1)}) %all-gather.14.cloned.1.call-update) | async-done | bytes 4194320 | tf_op jit(solution)/shard_map/while/body/eval_jaxpr/all_gather | solution.py:8
  1063.3 66.0 %all-gather.14.cloned.1.call-done = bf16[64,2,128,128]{3,2,1,0:T(8,128)(2,1)} async-done(((bf16[1,2,128,128]{3,2,1,0:T(8,128)(2,1)}), bf16[64,2,128,128]{3,2,1,0:T(8,128)(2,1)}) %all-gather.14.cloned.1.call-update) | async-done | bytes 4194320 | tf_op jit(solution)/shard_map/while/body/eval_jaxpr/all_gather | solution.py:8
  1133.8 66.0 %all-gather.14.cloned.1.call-done = bf16[64,2,128,128]{3,2,1,0:T(8,128)(2,1)} async-done(((bf16[1,2,128,128]{3,2,1,0:T(8,128)(2,1)}), bf16[64,2,128,128]{3,2,1,0:T(8,128)(2,1)}) %all-gather.14.cloned.1.call-update) | async-done | bytes 4194320 | tf_op jit(solution)/shard_map/while/body/eval_jaxpr/all_gather | solution.py:8
  1204.2 66.0 %all-gather.14.cloned.1.call-done = bf16[64,2,128,128]{3,2,1,0:T(8,128)(2,1)} async-done(((bf16[1,2,128,128]{3,2,1,0:T(8,128)(2,1)}), bf16[64,2,128,128]{3,2,1,0:T(8,128)(2,1)}) %all-gather.14.cloned.1.call-update) | async-done | bytes 4194320 | tf_op jit(solution)/shard_map/while/body/eval_jaxpr/all_gather | solution.py:8
  1274.7 66.0 %all-gather.14.cloned.1.call-done = bf16[64,2,128,128]{3,2,1,0:T(8,128)(2,1)} async-done(((bf16[1,2,128,128]{3,2,1,0:T(8,128)(2,1)}), bf16[64,2,128,128]{3,2,1,0:T(8,128)(2,1)}) %all-gather.14.cloned.1.call-update) | async-done | bytes 4194320 | tf_op jit(solution)/shard_map/while/body/eval_jaxpr/all_gather | solution.py:8
  1342.3 11.7 custom-call.36
  1355.4 9.8 custom-call.37
  1369.6 563.6 %while.89 = (s32[]{:T(128)}, f32[1,2,128,128]{3,2,1,0:T(8,128)S(1)}, f32[1,4,128,128]{3,2,1,0:T(8,128)S(1)}, f32[1,2,128,128]{3,2,1,0:T(8,128)S(1)}, s32[64]{0:T...) while((s32[]{:T(128)}, ...), condition=%wide.region_12.15_spmd.clone, body=%wide.region_11.14_spmd.clone.sunk | while | flops 425996 | bytes 14483734 | solution.py:97
  1372.7 64.7 %all-gather.16.cloned.1.call-done = bf16[64,2,128,128]{3,2,1,0:T(8,128)(2,1)} async-done(((bf16[1,2,128,128]{3,2,1,0:T(8,128)(2,1)}), bf16[64,2,128,128]{3,2,1,0:T(8,128)(2,1)}) %all-gather.16.cloned.1.call-update) | async-done | bytes 4194320 | tf_op jit(solution)/shard_map/while/body/eval_jaxpr/all_gather | solution.py:8
  1441.8 66.3 %all-gather.16.cloned.1.call-done = bf16[64,2,128,128]{3,2,1,0:T(8,128)(2,1)} async-done(((bf16[1,2,128,128]{3,2,1,0:T(8,128)(2,1)}), bf16[64,2,128,128]{3,2,1,0:T(8,128)(2,1)}) %all-gather.16.cloned.1.call-update) | async-done | bytes 4194320 | tf_op jit(solution)/shard_map/while/body/eval_jaxpr/all_gather | solution.py:8
  1512.4 66.2 %all-gather.16.cloned.1.call-done = bf16[64,2,128,128]{3,2,1,0:T(8,128)(2,1)} async-done(((bf16[1,2,128,128]{3,2,1,0:T(8,128)(2,1)}), bf16[64,2,128,128]{3,2,1,0:T(8,128)(2,1)}) %all-gather.16.cloned.1.call-update) | async-done | bytes 4194320 | tf_op jit(solution)/shard_map/while/body/eval_jaxpr/all_gather | solution.py:8
  1583.0 66.4 %all-gather.16.cloned.1.call-done = bf16[64,2,128,128]{3,2,1,0:T(8,128)(2,1)} async-done(((bf16[1,2,128,128]{3,2,1,0:T(8,128)(2,1)}), bf16[64,2,128,128]{3,2,1,0:T(8,128)(2,1)}) %all-gather.16.cloned.1.call-update) | async-done | bytes 4194320 | tf_op jit(solution)/shard_map/while/body/eval_jaxpr/all_gather | solution.py:8
  1653.8 66.3 %all-gather.16.cloned.1.call-done = bf16[64,2,128,128]{3,2,1,0:T(8,128)(2,1)} async-done(((bf16[1,2,128,128]{3,2,1,0:T(8,128)(2,1)}), bf16[64,2,128,128]{3,2,1,0:T(8,128)(2,1)}) %all-gather.16.cloned.1.call-update) | async-done | bytes 4194320 | tf_op jit(solution)/shard_map/while/body/eval_jaxpr/all_gather | solution.py:8
  1724.5 66.4 %all-gather.16.cloned.1.call-done = bf16[64,2,128,128]{3,2,1,0:T(8,128)(2,1)} async-done(((bf16[1,2,128,128]{3,2,1,0:T(8,128)(2,1)}), bf16[64,2,128,128]{3,2,1,0:T(8,128)(2,1)}) %all-gather.16.cloned.1.call-update) | async-done | bytes 4194320 | tf_op jit(solution)/shard_map/while/body/eval_jaxpr/all_gather | solution.py:8
  1795.1 66.2 %all-gather.16.cloned.1.call-done = bf16[64,2,128,128]{3,2,1,0:T(8,128)(2,1)} async-done(((bf16[1,2,128,128]{3,2,1,0:T(8,128)(2,1)}), bf16[64,2,128,128]{3,2,1,0:T(8,128)(2,1)}) %all-gather.16.cloned.1.call-update) | async-done | bytes 4194320 | tf_op jit(solution)/shard_map/while/body/eval_jaxpr/all_gather | solution.py:8
  1865.7 66.3 %all-gather.16.cloned.1.call-done = bf16[64,2,128,128]{3,2,1,0:T(8,128)(2,1)} async-done(((bf16[1,2,128,128]{3,2,1,0:T(8,128)(2,1)}), bf16[64,2,128,128]{3,2,1,0:T(8,128)(2,1)}) %all-gather.16.cloned.1.call-update) | async-done | bytes 4194320 | tf_op jit(solution)/shard_map/while/body/eval_jaxpr/all_gather | solution.py:8
  1933.6 11.7 custom-call.38
  1946.6 9.8 custom-call.39
  1960.8 280.8 %while.90 = (s32[]{:T(128)}, f32[1,2,128,128]{3,2,1,0:T(8,128)S(1)}, f32[1,4,128,128]{3,2,1,0:T(8,128)S(1)}, f32[1,2,128,128]{3,2,1,0:T(8,128)S(1)}, s32[64]{0:T...) while((s32[]{:T(128)}, ...), condition=%wide.region_15.18_spmd.clone, body=%wide.region_14.17_spmd.clone.sunk | while | flops 425996 | bytes 14483734 | solution.py:97
  1964.0 64.7 %all-gather.18.cloned.1.call-done = bf16[64,2,128,128]{3,2,1,0:T(8,128)(2,1)} async-done(((bf16[1,2,128,128]{3,2,1,0:T(8,128)(2,1)}), bf16[64,2,128,128]{3,2,1,0:T(8,128)(2,1)}) %all-gather.18.cloned.1.call-update) | async-done | bytes 4194320 | tf_op jit(solution)/shard_map/while/body/eval_jaxpr/all_gather | solution.py:8
  2032.9 66.2 %all-gather.18.cloned.1.call-done = bf16[64,2,128,128]{3,2,1,0:T(8,128)(2,1)} async-done(((bf16[1,2,128,128]{3,2,1,0:T(8,128)(2,1)}), bf16[64,2,128,128]{3,2,1,0:T(8,128)(2,1)}) %all-gather.18.cloned.1.call-update) | async-done | bytes 4194320 | tf_op jit(solution)/shard_map/while/body/eval_jaxpr/all_gather | solution.py:8
  2103.5 66.3 %all-gather.18.cloned.1.call-done = bf16[64,2,128,128]{3,2,1,0:T(8,128)(2,1)} async-done(((bf16[1,2,128,128]{3,2,1,0:T(8,128)(2,1)}), bf16[64,2,128,128]{3,2,1,0:T(8,128)(2,1)}) %all-gather.18.cloned.1.call-update) | async-done | bytes 4194320 | tf_op jit(solution)/shard_map/while/body/eval_jaxpr/all_gather | solution.py:8
  2174.3 66.4 %all-gather.18.cloned.1.call-done = bf16[64,2,128,128]{3,2,1,0:T(8,128)(2,1)} async-done(((bf16[1,2,128,128]{3,2,1,0:T(8,128)(2,1)}), bf16[64,2,128,128]{3,2,1,0:T(8,128)(2,1)}) %all-gather.18.cloned.1.call-update) | async-done | bytes 4194320 | tf_op jit(solution)/shard_map/while/body/eval_jaxpr/all_gather | solution.py:8
  2242.2 11.7 custom-call.40
  2269.3 139.7 %while.91 = (s32[]{:T(128)}, f32[1,2,128,128]{3,2,1,0:T(8,128)S(1)}, f32[1,4,128,128]{3,2,1,0:T(8,128)S(1)}, f32[1,2,128,128]{3,2,1,0:T(8,128)S(1)}, s32[64]{0:T...) while((s32[]{:T(128)}, ...), condition=%wide.region_18.21_spmd.clone, body=%wide.region_17.20_spmd.clone.sunk | while | flops 425996 | bytes 14483734 | solution.py:97
  2272.5 64.7 %all-gather.20.cloned.1.call-done = bf16[64,2,128,128]{3,2,1,0:T(8,128)(2,1)} async-done(((bf16[1,2,128,128]{3,2,1,0:T(8,128)(2,1)}), bf16[64,2,128,128]{3,2,1,0:T(8,128)(2,1)}) %all-gather.20.cloned.1.call-update) | async-done | bytes 4194320 | tf_op jit(solution)/shard_map/while/body/eval_jaxpr/all_gather | solution.py:8
  2341.6 66.4 %all-gather.20.cloned.1.call-done = bf16[64,2,128,128]{3,2,1,0:T(8,128)(2,1)} async-done(((bf16[1,2,128,128]{3,2,1,0:T(8,128)(2,1)}), bf16[64,2,128,128]{3,2,1,0:T(8,128)(2,1)}) %all-gather.20.cloned.1.call-update) | async-done | bytes 4194320 | tf_op jit(solution)/shard_map/while/body/eval_jaxpr/all_gather | solution.py:8
  2409.5 11.7 custom-call.42
  (418 shorter events, 166.9 us)
Async XLA Ops:
  7.2 131.5 %copy-start = (f32[1,1,128,128]{3,2,1,0:T(8,128)S(1)}, f32[1,1,128,128]{3,2,1,0:T(8,128)}, u32[]{:S(2)}) copy-start(f32[1,1,128,128]{3,2,1,0:T(8,128)} %param.18) | copy-start | bytes 196612
  7.2 107.0 %all-gather.12.cloned.1.call-start = ((), (), s32[]{:S(2)}) async-start(), calls=%async_computation.1 | async-start | bytes 4259840 | tf_op jit(solution)/shard_map/while/body/eval_jaxpr/all_gather | solution.py:8
  141.2 33.6 %all-to-all-start = ((bf16[64,1,128,128]{3,2,1,0:T(8,128)(2,1)}), bf16[64,1,128,128]{3,2,1,0:T(8,128)(2,1)S(1)}, u32[]{:S(2)}, u32[]{:S(2)}) async-start(bf16[64,1,128,128]{3,2,1,0:T(8,128)(2,1)} %broadcast_in_dim.256), calls=%async_computation | async-start | bytes 4194304 | tf_op jit(solution)/shard_map/all_to_all | solution.py:19
  177.5 12.0 collective-permute-start
  189.3 23.2 collective-permute-start.1
  215.3 66.9 %all-gather.14.cloned.1.call-start = ((), (), s32[]{:S(2)}) async-start(), calls=%async_computation.2 | async-start | bytes 4259840 | tf_op jit(solution)/shard_map/while/body/eval_jaxpr/all_gather | solution.py:8
  283.3 69.7 %all-gather.14.cloned.1.call-start = ((), (), s32[]{:S(2)}) async-start(), calls=%async_computation.2 | async-start | bytes 4259840 | tf_op jit(solution)/shard_map/while/body/eval_jaxpr/all_gather | solution.py:8
  354.1 69.4 %all-gather.14.cloned.1.call-start = ((), (), s32[]{:S(2)}) async-start(), calls=%async_computation.2 | async-start | bytes 4259840 | tf_op jit(solution)/shard_map/while/body/eval_jaxpr/all_gather | solution.py:8
  424.5 69.4 %all-gather.14.cloned.1.call-start = ((), (), s32[]{:S(2)}) async-start(), calls=%async_computation.2 | async-start | bytes 4259840 | tf_op jit(solution)/shard_map/while/body/eval_jaxpr/all_gather | solution.py:8
  494.9 69.4 %all-gather.14.cloned.1.call-start = ((), (), s32[]{:S(2)}) async-start(), calls=%async_computation.2 | async-start | bytes 4259840 | tf_op jit(solution)/shard_map/while/body/eval_jaxpr/all_gather | solution.py:8
  565.4 69.7 %all-gather.14.cloned.1.call-start = ((), (), s32[]{:S(2)}) async-start(), calls=%async_computation.2 | async-start | bytes 4259840 | tf_op jit(solution)/shard_map/while/body/eval_jaxpr/all_gather | solution.py:8
  636.1 69.7 %all-gather.14.cloned.1.call-start = ((), (), s32[]{:S(2)}) async-start(), calls=%async_computation.2 | async-start | bytes 4259840 | tf_op jit(solution)/shard_map/while/body/eval_jaxpr/all_gather | solution.py:8
  706.9 69.7 %all-gather.14.cloned.1.call-start = ((), (), s32[]{:S(2)}) async-start(), calls=%async_computation.2 | async-start | bytes 4259840 | tf_op jit(solution)/shard_map/while/body/eval_jaxpr/all_gather | solution.py:8
  777.6 69.4 %all-gather.14.cloned.1.call-start = ((), (), s32[]{:S(2)}) async-start(), calls=%async_computation.2 | async-start | bytes 4259840 | tf_op jit(solution)/shard_map/while/body/eval_jaxpr/all_gather | solution.py:8
  848.1 69.7 %all-gather.14.cloned.1.call-start = ((), (), s32[]{:S(2)}) async-start(), calls=%async_computation.2 | async-start | bytes 4259840 | tf_op jit(solution)/shard_map/while/body/eval_jaxpr/all_gather | solution.py:8
  918.8 69.4 %all-gather.14.cloned.1.call-start = ((), (), s32[]{:S(2)}) async-start(), calls=%async_computation.2 | async-start | bytes 4259840 | tf_op jit(solution)/shard_map/while/body/eval_jaxpr/all_gather | solution.py:8
  989.3 69.7 %all-gather.14.cloned.1.call-start = ((), (), s32[]{:S(2)}) async-start(), calls=%async_computation.2 | async-start | bytes 4259840 | tf_op jit(solution)/shard_map/while/body/eval_jaxpr/all_gather | solution.py:8
  1060.0 69.4 %all-gather.14.cloned.1.call-start = ((), (), s32[]{:S(2)}) async-start(), calls=%async_computation.2 | async-start | bytes 4259840 | tf_op jit(solution)/shard_map/while/body/eval_jaxpr/all_gather | solution.py:8
  1130.5 69.4 %all-gather.14.cloned.1.call-start = ((), (), s32[]{:S(2)}) async-start(), calls=%async_computation.2 | async-start | bytes 4259840 | tf_op jit(solution)/shard_map/while/body/eval_jaxpr/all_gather | solution.py:8
  1200.9 69.4 %all-gather.14.cloned.1.call-start = ((), (), s32[]{:S(2)}) async-start(), calls=%async_computation.2 | async-start | bytes 4259840 | tf_op jit(solution)/shard_map/while/body/eval_jaxpr/all_gather | solution.py:8
  1271.3 69.4 %all-gather.14.cloned.1.call-start = ((), (), s32[]{:S(2)}) async-start(), calls=%async_computation.2 | async-start | bytes 4259840 | tf_op jit(solution)/shard_map/while/body/eval_jaxpr/all_gather | solution.py:8
  1369.6 67.8 %all-gather.16.cloned.1.call-start = ((), (), s32[]{:S(2)}) async-start(), calls=%async_computation.3 | async-start | bytes 4259840 | tf_op jit(solution)/shard_map/while/body/eval_jaxpr/all_gather | solution.py:8
  1438.5 69.7 %all-gather.16.cloned.1.call-start = ((), (), s32[]{:S(2)}) async-start(), calls=%async_computation.3 | async-start | bytes 4259840 | tf_op jit(solution)/shard_map/while/body/eval_jaxpr/all_gather | solution.py:8
  1509.3 69.4 %all-gather.16.cloned.1.call-start = ((), (), s32[]{:S(2)}) async-start(), calls=%async_computation.3 | async-start | bytes 4259840 | tf_op jit(solution)/shard_map/while/body/eval_jaxpr/all_gather | solution.py:8
  1579.7 69.7 %all-gather.16.cloned.1.call-start = ((), (), s32[]{:S(2)}) async-start(), calls=%async_computation.3 | async-start | bytes 4259840 | tf_op jit(solution)/shard_map/while/body/eval_jaxpr/all_gather | solution.py:8
  1650.5 69.7 %all-gather.16.cloned.1.call-start = ((), (), s32[]{:S(2)}) async-start(), calls=%async_computation.3 | async-start | bytes 4259840 | tf_op jit(solution)/shard_map/while/body/eval_jaxpr/all_gather | solution.py:8
  1721.2 69.7 %all-gather.16.cloned.1.call-start = ((), (), s32[]{:S(2)}) async-start(), calls=%async_computation.3 | async-start | bytes 4259840 | tf_op jit(solution)/shard_map/while/body/eval_jaxpr/all_gather | solution.py:8
  1792.0 69.4 %all-gather.16.cloned.1.call-start = ((), (), s32[]{:S(2)}) async-start(), calls=%async_computation.3 | async-start | bytes 4259840 | tf_op jit(solution)/shard_map/while/body/eval_jaxpr/all_gather | solution.py:8
  1862.4 69.7 %all-gather.16.cloned.1.call-start = ((), (), s32[]{:S(2)}) async-start(), calls=%async_computation.3 | async-start | bytes 4259840 | tf_op jit(solution)/shard_map/while/body/eval_jaxpr/all_gather | solution.py:8
  1960.8 67.8 %all-gather.18.cloned.1.call-start = ((), (), s32[]{:S(2)}) async-start(), calls=%async_computation.4 | async-start | bytes 4259840 | tf_op jit(solution)/shard_map/while/body/eval_jaxpr/all_gather | solution.py:8
  2029.7 69.4 %all-gather.18.cloned.1.call-start = ((), (), s32[]{:S(2)}) async-start(), calls=%async_computation.4 | async-start | bytes 4259840 | tf_op jit(solution)/shard_map/while/body/eval_jaxpr/all_gather | solution.py:8
  2100.2 69.7 %all-gather.18.cloned.1.call-start = ((), (), s32[]{:S(2)}) async-start(), calls=%async_computation.4 | async-start | bytes 4259840 | tf_op jit(solution)/shard_map/while/body/eval_jaxpr/all_gather | solution.py:8
  2170.9 69.7 %all-gather.18.cloned.1.call-start = ((), (), s32[]{:S(2)}) async-start(), calls=%async_computation.4 | async-start | bytes 4259840 | tf_op jit(solution)/shard_map/while/body/eval_jaxpr/all_gather | solution.py:8
  2269.3 67.8 %all-gather.20.cloned.1.call-start = ((), (), s32[]{:S(2)}) async-start(), calls=%async_computation.5 | async-start | bytes 4259840 | tf_op jit(solution)/shard_map/while/body/eval_jaxpr/all_gather | solution.py:8
  2338.3 69.7 %all-gather.20.cloned.1.call-start = ((), (), s32[]{:S(2)}) async-start(), calls=%async_computation.5 | async-start | bytes 4259840 | tf_op jit(solution)/shard_map/while/body/eval_jaxpr/all_gather | solution.py:8
Sparse Core Ops, SparseCore 0:
  44.6 69.5 all-gather.11
  219.0 63.1 all-gather.13
  287.0 65.9 all-gather.13
  357.4 65.9 all-gather.13
  427.9 65.9 all-gather.13
  498.3 65.9 all-gather.13
  569.1 65.9 all-gather.13
  639.8 65.9 all-gather.13
  710.6 65.9 all-gather.13
  781.0 65.9 all-gather.13
  851.8 65.9 all-gather.13
  922.2 65.9 all-gather.13
  993.0 65.9 all-gather.13
  1063.4 65.9 all-gather.13
  1133.9 65.9 all-gather.13
  1204.3 65.9 all-gather.13
  1274.7 65.9 all-gather.13
  1373.0 64.4 all-gather.15
  1442.2 65.9 all-gather.15
  1512.6 65.9 all-gather.15
  1583.4 65.9 all-gather.15
  1654.2 65.9 all-gather.15
  1724.9 65.9 all-gather.15
  1795.3 65.9 all-gather.15
  1866.1 65.9 all-gather.15
  1964.2 64.4 all-gather.17
  2033.1 65.9 all-gather.17
  2103.9 65.9 all-gather.17
  2174.6 65.9 all-gather.17
  2272.7 64.4 all-gather.19
  2341.9 65.9 all-gather.19
where the time goes:
time: 2450 us
  waiting for transfers between devices  2090 us (85%)
  other arithmetic  212 us (9%)
  loops' own time  61.7 us (3%)
  local copies, waits for them, and re-layouts  29.8 us (1%)
    all_gather x31, waiting for transfers between devices, picked(): lax.all_gather(x, axis)  2040 us
    another operation x21, other arithmetic, shards(): lower = jnp.linalg.cholesky(acc_diag)  86.9 us
    another operation x14, other arithmetic, one(): return jax.scipy.linalg.solve_triangular(factor, block.T, lower=True).T  73.1 us
    another operation x4, loops' own time, spread_nodes(): return lax.fori_loop(0, present, visit, blanks)  61.7 us
  transfers between devices with their start and end apart: 34, of which 32 were waited for; matrix products, arithmetic and copies ran while one was open for 2% of the time, Pallas kernels for 0%

commit v1 on v0

v1 whole, which is shorter than its diff:
```python
import jax
import jax.numpy as jnp
from jax import lax
from jax.experimental import pallas as pl
from jax.experimental.pallas import tpu as pltpu
from jax.sharding import PartitionSpec as P

F32, BF16 = jnp.float32, jnp.bfloat16
MESH = pl.DeviceIdType.MESH
W = 128
NODES = 64
LEVELS = 7
BLOCK = 32
PART = 16


def order_kernel(targets, order, count, total, first):
    def clear(i, carry):
        count[i] = 0
        total[i] = 0
        return carry

    lax.fori_loop(0, NODES + 1, clear, 0)

    def enter(s, carry):
        p = targets[s, 0]
        count[p] = count[p] + 1
        total[p] = total[p] + s
        first[p] = s
        return carry

    lax.fori_loop(0, NODES, enter, 0)
    lone = lax.fori_loop(0, NODES, lambda s, x: jnp.where(count[s] == 1, s, x), 0)
    first[lone] = total[lone]
    node = lone
    for _ in range(LEVELS - 2):
        above = targets[node, 0]
        first[above] = node
        node = above
    order[0] = node
    order[NODES - 1] = total[lone]

    def descend(h, carry):
        node = order[h]
        order[2 * h + 1] = first[node]
        order[2 * h + 2] = total[node] - first[node]
        return carry

    lax.fori_loop(0, NODES // 2 - 1, descend, 0)

    def invert(h, carry):
        order[NODES + order[h]] = h
        return carry

    lax.fori_loop(0, NODES, invert, 0)


def heap_order(targets):
    return pl.pallas_call(
        order_kernel,
        out_shape=jax.ShapeDtypeStruct((2 * NODES,), jnp.int32),
        in_specs=[pl.BlockSpec(memory_space=pltpu.SMEM)],
        out_specs=pl.BlockSpec(memory_space=pltpu.SMEM),
        scratch_shapes=[pltpu.SMEM((NODES + 1,), jnp.int32)] * 3,
        name="heap_order",
    )(targets)


def in_three(x):
    high = x.astype(BF16)
    rest = x - high.astype(F32)
    middle = rest.astype(BF16)
    return high, middle, (rest - middle.astype(F32)).astype(BF16)


def wide(x, n):
    return jnp.concatenate([x] * n, axis=1)


def factor(work):
    tall = BLOCK // 8
    row = lax.broadcasted_iota(jnp.int32, (8, W), 0)
    for b in range(W // BLOCK):
        start = b * BLOCK
        x = [work[pl.ds(start + 8 * v, 8), :] for v in range(tall)]
        scale = [None] * tall
        for part in range(0, BLOCK, PART):
            cols = {}
            for k in range(part, part + PART):
                for v in range(k // 8, tall):
                    cols[k, v] = jnp.broadcast_to(x[v][:, start + k : start + k + 1], (8, W))
            for j in range(part, part + PART):
                v0, s = divmod(j, 8)
                r = lax.rsqrt(jnp.broadcast_to(cols[j, v0][s : s + 1, :], (8, W)))
                low = {v: cols[j, v] * r for v in range(v0, tall)}
                below = dict(low)
                below[v0] = jnp.where(row > s, low[v0], 0.0)
                scale[v0] = r if s == 0 else jnp.where(row == s, r, scale[v0])
                pivot = jnp.concatenate(
                    [
                        jnp.broadcast_to(x[v0][s : s + 1, c * W : (c + 1) * W], (8, W)) * r
                        for c in range(3)
                    ],
                    axis=1,
                )
                for k in range(j + 1, part + PART):
                    mult = jnp.broadcast_to(low[k // 8][k % 8 : k % 8 + 1, :], (8, W))
                    for v in range(k // 8, tall):
                        cols[k, v] = cols[k, v] - low[v] * mult
                for v in range(v0, tall):
                    x[v] = x[v] - wide(below[v], 3) * pivot
        for v in range(tall):
            x[v] = x[v] * wide(scale[v], 3)
            work[pl.ds(start + 8 * v, 8), :] = x[v]
        if start + BLOCK < W:
            high, middle, low3 = in_three(jnp.concatenate(x, axis=0))
            right = jnp.concatenate([high, middle, high, low3, middle, high], axis=0)
            left = jnp.concatenate(
                [p[:, :W] for p in (high, high, middle, high, middle, low3)], axis=0
            )
            update = jnp.dot(left.T[start + BLOCK :, :], right, preferred_element_type=F32)
            work[pl.ds(start + BLOCK, W - start - BLOCK), :] -= update


def tree_kernel(
    order,
    diag,
    panel,
    out_diag,
    out_panel,
    by_label,
    by_place,
    back_place,
    back_label,
    held,
    done,
    work,
    kids,
    kids_out,
    spare,
    spare_in,
    spare_out,
    send1,
    recv1,
    send2,
    recv2,
    send_kids,
    recv_kids,
    send_spare,
    recv_spare,
    send3,
    recv3,
    send4,
    recv_diag,
    recv_panel,
):
    col = lax.axis_index("col")
    grp = lax.axis_index("grp")
    y, x, z = col // 16, (col // 4) % 4, col % 4
    passes = (y // 2 + x // 2) == 1
    tile = (y // 2) * 16 + (y % 2) * 8 + (x % 2) * 4 + z
    works = (y // 2 + x // 2) == 0
    role = (1 - grp) + 2 * (z % 2) + 4 * x + 8 * y + 16 * (z // 2)

    def copy(src, dst, send, recv, to):
        return pltpu.make_async_remote_copy(
            src_ref=src, dst_ref=dst, send_sem=send, recv_sem=recv, device_id=to, device_id_type=MESH
        )

    def passer(t, g):
        h = t // 16
        py, px = 2 * h + (t // 8) % 2, 2 * (1 - h) + (t // 4) % 2
        return (py * 16 + px * 4 + t % 4, g)

    def worker(r):
        wz, wx, wy = (r // 2) % 2 + 2 * (r // 16), (r // 4) % 2, (r // 8) % 2
        return (wy * 16 + wx * 4 + wz, 1 - r % 2)

    def rows(n):
        return pl.ds(pl.multiple_of(n * 8, 8), 8)

    def spread(t, carry):
        copy(diag.at[0, rows(t)], by_label.at[col], send1, recv1, passer(t, 1 - grp)).start()
        copy(panel.at[0, 0, rows(t)], by_label.at[col], send1, recv1, passer(16 + t, 1 - grp)).start()
        return carry

    lax.fori_loop(0, 16, spread, 0)

    @pl.when(works)
    def _():
        kids[0] = jnp.zeros((2, 2 * W, W), BF16)
        spare[...] = jnp.zeros((W, W), F32)
        spare_in[0] = jnp.zeros((W, W), F32)

    on_diag = tile < 16
    sends_in = passes & ((tile >= 16) | ((tile < 8) == (grp == 1)))
    held_row = jnp.where(on_diag, tile, 16 + 16 * (1 - grp) + tile - 16)

    @pl.when(passes)
    def _():
        pltpu.make_async_copy(by_label, by_label, recv1).wait()

    @pl.when(sends_in)
    def _():
        def place(h, carry):
            by_place[h] = by_label[order[h]]
            return carry

        lax.fori_loop(0, NODES, place, 0)
        for step in range(LEVELS):
            first = (1 << (6 - step)) - 1
            stride = 1 << max(step - 1, 0)

            def hand_in(i, carry):
                copy(
                    by_place.at[first + i],
                    held.at[step, rows(held_row)],
                    send2,
                    recv2.at[step],
                    worker(i * stride),
                ).start()
                return carry

            lax.fori_loop(0, 1 if step == 0 else first + 1, hand_in, 0)

    def active(step, stride):
        return (role % stride == 0) & ((step > 0) | (role == 0))

    def climb(step, carry):
        stride, first = carry

        @pl.when(active(step, stride))
        def _():
            prev = jnp.maximum(step - 1, 0)
            gives = (role // stride) % 2 == 1
            partner = worker(jnp.maximum(role - stride, 0))
            pltpu.make_async_copy(held.at[step], held.at[step], recv2.at[step]).wait()
            work[:, W : 2 * W] = held[step, W : 2 * W, :].T
            work[:, 2 * W :] = held[step, 2 * W :, :].T

            @pl.when(step > 1)
            def _():
                pltpu.make_async_copy(kids.at[prev, 1], kids.at[prev, 1], recv_kids.at[prev]).wait()
                pltpu.make_async_copy(spare_in.at[prev], spare_in.at[prev], recv_spare.at[prev]).wait()

            near = jnp.concatenate([kids[prev, 0, :W, :], kids[prev, 1, :W, :]], axis=0)
            far = jnp.concatenate([kids[prev, 0, W:, :], kids[prev, 1, W:, :]], axis=0)
            both = jnp.concatenate([near, far], axis=1)
            update = jnp.dot(near.T, both, preferred_element_type=F32)
            ahead = jnp.dot(far.T, far, preferred_element_type=F32)
            work[:, :W] = held[step, :W, :] - (update[:, :W] + (spare[...] + spare_in[prev]))
            work[:, W : 2 * W] -= update[:, W:]

            @pl.when(gives)
            def _():
                spare_out[...] = ahead
                copy(spare_out, spare_in.at[step], send_spare, recv_spare.at[step], partner).start()

            @pl.when(jnp.logical_not(gives))
            def _():
                spare[...] = ahead

            factor(work)

            @pl.when(gives)
            def _():
                kids_out[:W, :] = work[:, W : 2 * W].astype(BF16)
                kids_out[W:, :] = work[:, 2 * W :].astype(BF16)
                copy(kids_out, kids.at[step, 1], send_kids, recv_kids.at[step], partner).start()

            @pl.when(jnp.logical_not(gives))
            def _():
                kids[step, 0, :W, :] = work[:, W : 2 * W].astype(BF16)
                kids[step, 0, W:, :] = work[:, 2 * W :].astype(BF16)

            down = lax.broadcasted_iota(jnp.int32, (W, W), 0)
            across = lax.broadcasted_iota(jnp.int32, (W, W), 1)
            done[step, :W, :] = jnp.where(across >= down, work[:, :W], 0.0).T
            done[step, W : 2 * W, :] = work[:, W : 2 * W].T
            done[step, 2 * W :, :] = work[:, 2 * W :].T
            place = first + role // stride

            def hand_out(t, carry):
                for g in range(2):
                    copy(
                        done.at[step, rows(t)],
                        back_place.at[place],
                        send3.at[step],
                        recv3,
                        passer(t, g),
                    ).start()
                    copy(
                        done.at[step, rows(16 + 16 * g + t)],
                        back_place.at[place],
                        send3.at[step],
                        recv3,
                        passer(16 + t, 1 - g),
                    ).start()
                return carry

            lax.fori_loop(0, 16, hand_out, 0)

        return jnp.where(step == 0, 1, stride * 2), first // 2

    @pl.when(works)
    def _():
        lax.fori_loop(0, LEVELS, climb, (1, NODES - 1))

    @pl.when(passes)
    def _():
        pltpu.make_async_copy(back_place, back_place, recv3).wait()

        def unplace(s, carry):
            back_label[s] = back_place[order[NODES + s]]
            return carry

        lax.fori_loop(0, NODES, unplace, 0)

    @pl.when(passes & on_diag)
    def _():
        def hand_back(s, carry):
            copy(back_label.at[s], out_diag.at[0, rows(tile)], send4, recv_diag, (s, 1 - grp)).start()
            return carry

        lax.fori_loop(0, NODES, hand_back, 0)

    @pl.when(passes & jnp.logical_not(on_diag))
    def _():
        def hand_back(s, carry):
            copy(
                back_label.at[s], out_panel.at[0, 0, rows(tile - 16)], send4, recv_panel, (s, 1 - grp)
            ).start()
            return carry

        lax.fori_loop(0, NODES, hand_back, 0)

    sent = by_label.at[pl.ds(0, 32)]
    pltpu.make_async_copy(sent, sent, send1).wait()

    @pl.when(sends_in)
    def _():
        pltpu.make_async_copy(by_place, by_place, send2).wait()

    @pl.when(works)
    def _():
        def drain(step, stride):
            @pl.when(active(step, stride))
            def _():
                pltpu.make_async_copy(by_label, by_label, send3.at[step]).wait()

            return jnp.where(step == 0, 1, stride * 2)

        lax.fori_loop(0, LEVELS, drain, 1)

        @pl.when(role > 0)
        def _():
            pltpu.make_async_copy(kids_out, kids_out, send_kids).wait()
            pltpu.make_async_copy(spare_out, spare_out, send_spare).wait()

    @pl.when(passes)
    def _():
        pltpu.make_async_copy(back_label, back_label, send4).wait()

    pltpu.make_async_copy(out_diag, out_diag, recv_diag).wait()
    pltpu.make_async_copy(out_panel, out_panel, recv_panel).wait()


def shards(diag_blocks, panel_blocks, targets):
    vmem = pl.BlockSpec(memory_space=pltpu.VMEM)
    dma = pltpu.SemaphoreType.DMA
    tiles = pltpu.VMEM((NODES, 8, W), F32)
    return pl.pallas_call(
        tree_kernel,
        out_shape=(
            jax.ShapeDtypeStruct(diag_blocks.shape, F32),
            jax.ShapeDtypeStruct(panel_blocks.shape, F32),
        ),
        in_specs=[pl.BlockSpec(memory_space=pltpu.SMEM), vmem, vmem],
        out_specs=(vmem, vmem),
        scratch_shapes=[
            tiles,
            tiles,
            tiles,
            tiles,
            pltpu.VMEM((LEVELS, 3 * W, W), F32),
            pltpu.VMEM((LEVELS, 3 * W, W), F32),
            pltpu.VMEM((W, 3 * W), F32),
            pltpu.VMEM((LEVELS, 2, 2 * W, W), BF16),
            pltpu.VMEM((2 * W, W), BF16),
            pltpu.VMEM((W, W), F32),
            pltpu.VMEM((LEVELS, W, W), F32),
            pltpu.VMEM((W, W), F32),
            dma,
            dma,
            dma,
            dma((LEVELS,)),
            dma,
            dma((LEVELS,)),
            dma,
            dma((LEVELS,)),
            dma((LEVELS,)),
            dma,
            dma,
            dma,
            dma,
        ],
        compiler_params=pltpu.CompilerParams(has_side_effects=True),
        name="tree",
    )(heap_order(targets), diag_blocks, panel_blocks)


def solution(mesh):
    placed = (P("col", None, None), P("col", "grp", None, None), P())
    return jax.shard_map(
        shards,
        mesh=mesh,
        in_specs=placed,
        out_specs=(P("col", None, None), P("col", "grp", None, None)),
        check_vma=False,
    )
```

time: 2450 us -> 84.1 us (0.03)
  waiting for transfers between devices: 2090 us -> 0 us
  other arithmetic: 212 us -> 0 us
  Pallas kernels: 0 us -> 79 us
  loops' own time: 61.7 us -> 0 us
  local copies, waits for them, and re-layouts: 29.8 us -> 3.52 us
    all_gather x31 -> x0, waiting for transfers between devices: 2040 us -> none  [picked(): lax.all_gather(x, axis)]
    another operation x36 -> x0, other arithmetic: 161 us -> none  [the longest x21 86.9 us: shards(): lower = jnp.linalg.cholesky(acc_diag)]
    pallas_call x0 -> x2, Pallas kernels: none -> 79 us  [the longest x1 74.4 us: shards(): pl.pallas_call(tree_kernel, out_shape=(jax.ShapeDtypeStruct(diag_blocks.s...]
    another operation x5 -> x0, loops' own time: 61.7 us -> none  [the longest x4 61.7 us: spread_nodes(): return lax.fori_loop(0, present, visit, blanks)]
    convert_element_type x101 -> x0, other arithmetic: 28.7 us -> none  [the longest x31 26.3 us: visit(): arrived = picked(piece, 'col', node // slots).astype(jnp.float32)]
    all_to_all x1 -> x0, waiting for transfers between devices: 27.1 us -> none  [sent_to_all(): return lax.all_to_all(copies, axis, split_axis=0, concat_axis=0, tiled=True)]
  transfers between devices with their start and end apart: 34 -> 0, of which waited for: 32 -> 0; matrix products, arithmetic and copies ran while one was open for 2% -> 0% of each run, Pallas kernels for 0% -> 0%
where the time goes in v1:
time: 84.1 us; the launch traced here: 83.2 us
  Pallas kernels  79 us (94%)
  local copies, waits for them, and re-layouts  3.52 us (4%)
    pallas_call x1, Pallas kernels, shards(): pl.pallas_call(tree_kernel, out_shape=(jax.ShapeDtypeStruct(diag_blocks.s...  74.4 us
    pallas_call x1, Pallas kernels, heap_order(): pl.pallas_call(order_kernel, out_shape=jax.ShapeDtypeStruct((2 * NODES,),...  4.61 us
    unnamed x5, local copies, waits for them, and re-layouts  3.52 us

profile of v1, /device:TPU:1, one launch (start us, length us, event | category | flops | bytes accessed | tf_op | source)
XLA Modules:
  0.0 83.2 jit_solution(6313690249007729965)
XLA Ops:
  0.6 1.4 %copy.5.targets = s32[64,2]{1,0:T(8,128)} copy(s32[64,2]{0,1:T(2,128)} %param.5) | data formatting | bytes 1024 | tf_op args[2]
  2.0 4.6 %heap_order.1.order = s32[128]{0:T(128)} custom-call(s32[64,2]{1,0:T(8,128)} %copy.5.targets), custom_call_target="tpu_custom_call" | custom-call | tf_op jit(solution)/shard_map/heap_order/pallas_call | solution.py:59
  6.6 74.4 %tree.1 = (f32[1,128,128]{2,1,0:T(8,128)}, f32[1,1,128,128]{3,2,1,0:T(8,128)}) custom-call(s32[128]{0:T(128)} %heap_order.1.order, f32[1,128,128]{2,1,0:T(8,128)} %diag.1, f32[1,1,128,128]{3,2,1,0:T(8,128)} %panel.1), custom_call_target="tpu_custom_call" | custom-call | tf_op jit(solution)/shard_map/tree/pallas_call | solution.py:372
  81.0 0.0 copy-start
  81.1 1.5 %copy.8 = f32[1,128,128]{2,1,0:T(8,128)} copy(f32[1,128,128]{2,1,0:T(8,128)} %get-tuple-element.4) | data formatting | bytes 131072
  82.6 0.0 copy-done
  82.6 0.6 copy.9
Async XLA Ops:
  81.0 1.5 %copy-start = (f32[1,1,128,128]{3,2,1,0:T(8,128)S(1)}, f32[1,1,128,128]{3,2,1,0:T(8,128)}, u32[]{:S(2)}) copy-start(f32[1,1,128,128]{3,2,1,0:T(8,128)} %get-tuple-element.5) | copy-start | bytes 196612

commit v2 on v1

v2 whole, which is shorter than its diff:
```python
import jax
import jax.numpy as jnp
from jax import lax
from jax.experimental import pallas as pl
from jax.experimental.pallas import tpu as pltpu
from jax.sharding import PartitionSpec as P

F32, BF16 = jnp.float32, jnp.bfloat16
MESH = pl.DeviceIdType.MESH
W = 128
NODES = 64
LEVELS = 7
BLOCK = 32
NEAR_FIRST = tuple(
    tuple(sorted(range(NODES), key=lambda s: (s // 16 + s // 4 % 4 + s % 4, (s * 7 + 16 * turn) % NODES)))
    for turn in range(4)
)
PART = 16


def power_of_two(n, most):
    result = jnp.ones_like(n)
    for k in range(1, most + 1):
        result = result * jnp.where(n >= k, 2.0, 1.0)
    return result


def heap_order(parent):
    def dot(a, b, over):
        return lax.dot_general(
            a.astype(BF16), b.astype(BF16), ((over[:1], over[1:]), ((), ())), preferred_element_type=F32
        )

    down = lax.broadcasted_iota(jnp.int32, (NODES, NODES), 0)
    across = lax.broadcasted_iota(jnp.int32, (NODES, NODES), 1)
    one = (down == parent).astype(F32)
    two = dot(one, one, (1, 0))
    four = dot(two, two, (1, 0))
    alive = jnp.broadcast_to((parent < NODES).astype(F32), (8, NODES))
    len2 = alive + dot(alive, one, (1, 0))
    len4 = len2 + dot(len2, two, (1, 0))
    depth = len4 + dot(len4, four, (1, 0))
    path = (depth == LEVELS - 1).astype(F32)
    for above in (one, two, four):
        path = path + dot(path, above, (1, 1))
    siblings = dot(one, one, (0, 0))
    rank = jnp.sum(jnp.where(down < across, siblings, 0.0), axis=0, keepdims=True)
    beside = dot(path, siblings, (1, 0)) - path * alive
    code = alive * (1.0 - path) * jnp.maximum(beside, rank)
    code = code + (1.0 + alive) * dot(code, one, (1, 0))
    code = code + power_of_two(len2, 2) * dot(code, two, (1, 0))
    code = code + power_of_two(len4, 4) * dot(code, four, (1, 0))
    place = power_of_two(depth, LEVELS - 1) - 1.0 + code
    holds = (down == jnp.broadcast_to(place[:1], (NODES, NODES)).astype(jnp.int32)).astype(F32)
    label = lax.broadcasted_iota(jnp.int32, (8, NODES), 1).astype(F32)
    return dot(label, holds, (1, 1)), place


def in_three(x):
    high = x.astype(BF16)
    rest = x - high.astype(F32)
    middle = rest.astype(BF16)
    return high, middle, (rest - middle.astype(F32)).astype(BF16)


def wide(x, n):
    return jnp.concatenate([x] * n, axis=1)


def factor(work, before_last):
    tall = BLOCK // 8
    row = lax.broadcasted_iota(jnp.int32, (8, W), 0)
    for b in range(W // BLOCK):
        start = b * BLOCK
        if start + BLOCK == W:
            before_last()
        x = [work[pl.ds(start + 8 * v, 8), :] for v in range(tall)]
        scale = [None] * tall
        for part in range(0, BLOCK, PART):
            cols = {}
            for k in range(part, part + PART):
                for v in range(k // 8, tall):
                    cols[k, v] = jnp.broadcast_to(x[v][:, start + k : start + k + 1], (8, W))
            for j in range(part, part + PART):
                v0, s = divmod(j, 8)
                r = lax.rsqrt(jnp.broadcast_to(cols[j, v0][s : s + 1, :], (8, W)))
                low = {v: cols[j, v] * r for v in range(v0, tall)}
                below = dict(low)
                below[v0] = jnp.where(row > s, low[v0], 0.0)
                scale[v0] = r if s == 0 else jnp.where(row == s, r, scale[v0])
                pivot = jnp.concatenate(
                    [
                        jnp.broadcast_to(x[v0][s : s + 1, c * W : (c + 1) * W], (8, W)) * r
                        for c in range(3)
                    ],
                    axis=1,
                )
                for k in range(j + 1, part + PART):
                    mult = jnp.broadcast_to(low[k // 8][k % 8 : k % 8 + 1, :], (8, W))
                    for v in range(k // 8, tall):
                        cols[k, v] = cols[k, v] - low[v] * mult
                for v in range(v0, tall):
                    x[v] = x[v] - wide(below[v], 3) * pivot
        for v in range(tall):
            x[v] = x[v] * wide(scale[v], 3)
            work[pl.ds(start + 8 * v, 8), :] = x[v]
        if start + BLOCK < W:
            high, middle, low3 = in_three(jnp.concatenate(x, axis=0))
            right = jnp.concatenate([high, middle, high, low3, middle, high], axis=0)
            left = jnp.concatenate(
                [p[:, :W] for p in (high, high, middle, high, middle, low3)], axis=0
            )
            update = jnp.dot(left.T[start + BLOCK :, :], right, preferred_element_type=F32)
            work[pl.ds(start + BLOCK, W - start - BLOCK), :] -= update


def tree_kernel(
    targets_in,
    diag_in,
    panel_in,
    out_diag,
    out_panel,
    targets,
    diag,
    panel,
    ranks,
    order,
    load,
    by_label,
    by_place,
    back_place,
    back_label,
    held,
    done,
    work,
    kids,
    kids_out,
    spare,
    spare_in,
    spare_out,
    send1,
    recv1,
    send2,
    recv2,
    send_kids,
    recv_kids,
    send_spare,
    recv_spare,
    send3,
    recv3,
    send4,
    recv_diag,
    recv_panel,
):
    col = lax.axis_index("col")
    grp = lax.axis_index("grp")
    y, x, z = col // 16, (col // 4) % 4, col % 4
    upper_y, upper_x = y // 2, x // 2
    works = (upper_y + upper_x) == 0
    role = (1 - grp) + 2 * (z % 2) + 4 * x + 8 * y + 16 * (z // 2)
    tile = (y % 2) * 8 + (x % 2) * 4 + z
    on_diag = (upper_y + upper_x) == 2
    on_panel = ((upper_y + upper_x) == 1) & (upper_x == grp)
    passes_in = on_panel | (on_diag & ((tile < 8) == (grp == 1)))
    passes_back = on_panel | on_diag
    kind = upper_x + 2 * upper_y
    held_row = tile + 16 * (kind % 3)

    def at(dy, dx, t):
        return (2 * dy + t // 8) * 16 + (2 * dx + (t // 4) % 2) * 4 + t % 4

    def diag_passer(t, g):
        return (at(1, 1, t), g)

    def panel_passer(t, c):
        return (at(c, 1 - c, t), 1 - c)

    def worker(r):
        wz, wx, wy = (r // 2) % 2 + 2 * (r // 16), (r // 4) % 2, (r // 8) % 2
        return (wy * 16 + wx * 4 + wz, 1 - r % 2)

    def within(n):
        return jnp.minimum(jnp.maximum(n, 0), NODES - 1)

    def rows(n):
        return pl.ds(pl.multiple_of(n * 8, 8), 8)

    def copy(src, dst, send, recv, to):
        return pltpu.make_async_remote_copy(
            src_ref=src, dst_ref=dst, send_sem=send, recv_sem=recv, device_id=to, device_id_type=MESH
        )

    def repeat(n, body, group=4):
        def several(i, carry):
            for k in range(group):
                body(i * group + k)
            return carry

        lax.fori_loop(0, n // group, several, 0)

    loads = [
        pltpu.make_async_copy(src, dst, load.at[k])
        for k, (src, dst) in enumerate(((targets_in, targets), (diag_in, diag), (panel_in, panel)))
    ]
    for one in loads:
        one.start()

    barrier = pltpu.get_barrier_semaphore()

    def greet(to):
        pl.semaphore_signal(barrier, inc=1, device_id=to, device_id_type=MESH)

    @pl.when(passes_in)
    def _():
        for s in NEAR_FIRST[0]:
            greet((s, 1 - grp))

    for g in range(2):

        @pl.when(works & (grp == g))
        def _(g=g):
            for t in range(16):
                greet(panel_passer(t, 1 - g))
                if (t < 8) == (g == 1):
                    greet(diag_passer(t, g))

    @pl.when(works)
    def _():
        kids[0] = jnp.zeros((2, W, 2 * W), BF16)
        spare[...] = jnp.zeros((W, W), F32)
        spare_in[0] = jnp.zeros((W, W), F32)

    loads[0].wait()

    @pl.when(passes_back)
    def _():
        with jax.named_scope("order"):
            node, place = heap_order(targets[0:1, :])
            ranks[:, :NODES] = node.astype(jnp.int32)
            ranks[:, NODES:] = place.astype(jnp.int32)
            to_scalar = pltpu.make_async_copy(ranks, order, load.at[3])
            to_scalar.start()
            to_scalar.wait()

    loads[1].wait()
    loads[2].wait()
    with jax.named_scope("barrier"):
        pl.semaphore_wait(barrier, 24 + jnp.where(passes_in, 16, 0))

    def spread_panel(i):
        t = (i + col) % 16
        copy(
            panel.at[0, 0, rows(t)], by_label.at[col], send1, recv1, (at(grp, 1 - grp, t), 1 - grp)
        ).start()

    def spread_diag(i):
        t = 8 * grp + (i + col) % 8
        copy(diag.at[0, rows(t)], by_label.at[col], send1, recv1, diag_passer(t, 1 - grp)).start()

    with jax.named_scope("spread"):
        repeat(8, spread_diag)
        repeat(16, spread_panel)

    @pl.when(passes_in)
    def _():
        with jax.named_scope("wait1"):
            pltpu.make_async_copy(by_label, by_label, recv1).wait()

        def place(h):
            by_place[h] = by_label[within(order[0, h])]

        repeat(NODES, place, 8)

        def hand_in(step, h, r):
            copy(
                by_place.at[h], held.at[step, rows(held_row)], send2.at[step // 2], recv2.at[step], worker(r)
            ).start()

        with jax.named_scope("handin"):
            hand_in(0, NODES - 1, 0)
            for turn in range(4):

                @pl.when((tile + kind) % 4 == turn)
                def _(turn=turn):
                    for i in range(32):
                        r = (i + 8 * turn) % 32
                        hand_in(1, 31 + r, r)

            first = by_place.at[pl.ds(0, 33)]
            pltpu.make_async_copy(first, first, send2.at[0]).wait()
            for step in range(2, LEVELS):
                count = 1 << (6 - step)
                for r in range(count):
                    hand_in(step, count - 1 + r, r << (step - 1))

    def active(step, stride):
        return (role % stride == 0) & ((step > 0) | (role == 0))

    def climb(step, carry):
        stride, first = carry

        @pl.when(active(step, stride))
        def _():
            prev = jnp.maximum(step - 1, 0)
            gives = (role // stride) % 2 == 1
            partner = worker(jnp.maximum(role - stride, 0))
            with jax.named_scope("waitheld"):
                pltpu.make_async_copy(held.at[step], held.at[step], recv2.at[step]).wait()
            work[:, W : 2 * W] = held[step, W : 2 * W, :].T
            work[:, 2 * W :] = held[step, 2 * W :, :].T

            @pl.when(step > 1)
            def _():
                with jax.named_scope("waitkids"):
                    pltpu.make_async_copy(spare_in.at[prev], spare_in.at[prev], recv_spare.at[prev]).wait()
                    for part in range(2):
                        lines = kids.at[prev, 1, pl.ds(96 * part, 96 - 64 * part)]
                        pltpu.make_async_copy(lines, lines, recv_kids.at[prev, part]).wait()

            both = jnp.concatenate([kids[prev, 0], kids[prev, 1]], axis=0)
            update = jnp.dot(both[:, :W].T, both, preferred_element_type=F32)
            work[:, :W] = held[step, :W, :] - (update[:, :W] + (spare[...] + spare_in[prev]))
            work[:, W : 2 * W] -= update[:, W:]
            ahead = jnp.dot(both[:, W:].T, both[:, W:], preferred_element_type=F32)

            @pl.when(gives)
            def _():
                spare_out[...] = ahead
                copy(spare_out, spare_in.at[step], send_spare, recv_spare.at[step], partner).start()

            @pl.when(jnp.logical_not(gives))
            def _():
                spare[...] = ahead

            def give(part):
                lines = pl.ds(96 * part, 96 - 64 * part)

                @pl.when(gives)
                def _():
                    kids_out[lines, :] = work[lines, W:].astype(BF16)
                    copy(
                        kids_out.at[lines],
                        kids.at[step, 1, lines],
                        send_kids.at[part],
                        recv_kids.at[step, part],
                        partner,
                    ).start()

            with jax.named_scope("factor"):
                factor(work, lambda: give(0))
            give(1)

            @pl.when(jnp.logical_not(gives))
            def _():
                kids[step, 0] = work[:, W:].astype(BF16)

            down = lax.broadcasted_iota(jnp.int32, (W, W), 0)
            across = lax.broadcasted_iota(jnp.int32, (W, W), 1)
            done[step, :W, :] = jnp.where(across >= down, work[:, :W], 0.0).T
            done[step, W : 2 * W, :] = work[:, W : 2 * W].T
            done[step, 2 * W :, :] = work[:, 2 * W :].T
            place = first + role // stride

            def hand_out(row, to):
                copy(
                    done.at[step, pl.ds(8 * row, 8)], back_place.at[place], send3.at[step], recv3, to
                ).start()

            with jax.named_scope("handout"):
                for t in range(16):
                    for g in range(2):
                        hand_out(t, diag_passer(t, g))
                        hand_out(16 + 16 * g + t, panel_passer(t, g))

        return jnp.where(step == 0, 1, stride * 2), first // 2

    @pl.when(works)
    def _():
        lax.fori_loop(0, LEVELS, climb, (1, NODES - 1))

    @pl.when(passes_back)
    def _():
        with jax.named_scope("wait3"):
            pltpu.make_async_copy(back_place, back_place, recv3).wait()

        def unplace(s):
            back_label[s] = back_place[within(order[0, NODES + s])]

        repeat(NODES, unplace, 8)

    def hand_back(s, to, recv):
        copy(back_label.at[s], to, send4, recv, (s, 1 - grp)).start()

    for turn in range(4):

        @pl.when(on_diag & (tile % 4 == turn))
        def _(turn=turn):
            for s in NEAR_FIRST[turn]:
                hand_back(s, out_diag.at[0, rows(tile)], recv_diag)

        @pl.when(on_panel & (tile % 4 == turn))
        def _(turn=turn):
            for s in NEAR_FIRST[turn]:
                hand_back(s, out_panel.at[0, 0, rows(tile)], recv_panel)

    sent = by_label.at[pl.ds(0, 24)]
    pltpu.make_async_copy(sent, sent, send1).wait()

    @pl.when(passes_in)
    def _():
        for step in range(1, 4):
            count = (0, 24, 6, 1)[step]
            later = by_place.at[pl.ds(0, count)]
            pltpu.make_async_copy(later, later, send2.at[step]).wait()

    @pl.when(works)
    def _():
        def drain(step, stride):
            @pl.when(active(step, stride))
            def _():
                pltpu.make_async_copy(by_label, by_label, send3.at[step]).wait()

            return jnp.where(step == 0, 1, stride * 2)

        lax.fori_loop(0, LEVELS, drain, 1)

        @pl.when(role > 0)
        def _():
            for part in range(2):
                lines = kids_out.at[pl.ds(96 * part, 96 - 64 * part)]
                pltpu.make_async_copy(lines, lines, send_kids.at[part]).wait()
            pltpu.make_async_copy(spare_out, spare_out, send_spare).wait()

    @pl.when(passes_back)
    def _():
        pltpu.make_async_copy(back_label, back_label, send4).wait()

    with jax.named_scope("waitfinal"):
        pltpu.make_async_copy(out_diag, out_diag, recv_diag).wait()
        pltpu.make_async_copy(out_panel, out_panel, recv_panel).wait()


def shards(diag_blocks, panel_blocks, targets):
    dma = pltpu.SemaphoreType.DMA
    tiles = pltpu.VMEM((NODES, 8, W), F32)
    return pl.pallas_call(
        tree_kernel,
        out_shape=(
            jax.ShapeDtypeStruct(diag_blocks.shape, F32),
            jax.ShapeDtypeStruct(panel_blocks.shape, F32),
        ),
        in_specs=[pl.BlockSpec(memory_space=pl.ANY)] * 3,
        out_specs=(pl.BlockSpec(memory_space=pltpu.VMEM),) * 2,
        scratch_shapes=[
            pltpu.VMEM((2, NODES), jnp.int32),
            pltpu.VMEM(diag_blocks.shape, F32),
            pltpu.VMEM(panel_blocks.shape, F32),
            pltpu.VMEM((8, 2 * NODES), jnp.int32),
            pltpu.SMEM((8, 2 * NODES), jnp.int32),
            dma((4,)),
            tiles,
            tiles,
            tiles,
            tiles,
            pltpu.VMEM((LEVELS, 3 * W, W), F32),
            pltpu.VMEM((LEVELS, 3 * W, W), F32),
            pltpu.VMEM((W, 3 * W), F32),
            pltpu.VMEM((LEVELS, 2, W, 2 * W), BF16),
            pltpu.VMEM((W, 2 * W), BF16),
            pltpu.VMEM((W, W), F32),
            pltpu.VMEM((LEVELS, W, W), F32),
            pltpu.VMEM((W, W), F32),
            dma,
            dma,
            dma((4,)),
            dma((LEVELS,)),
            dma((2,)),
            dma((LEVELS, 2)),
            dma,
            dma((LEVELS,)),
            dma((LEVELS,)),
            dma,
            dma,
            dma,
            dma,
        ],
        compiler_params=pltpu.CompilerParams(collective_id=0, has_side_effects=True),
        name="tree",
    )(targets.T, diag_blocks, panel_blocks)


def solution(mesh):
    placed = (P("col", None, None), P("col", "grp", None, None), P())
    return jax.shard_map(
        shards,
        mesh=mesh,
        in_specs=placed,
        out_specs=(P("col", None, None), P("col", "grp", None, None)),
        check_vma=False,
    )
```

time: 84.1 us -> 68.2 us (0.81)
  Pallas kernels: 79 us -> 65.2 us
  local copies, waits for them, and re-layouts: 3.52 us -> 2.14 us
    pallas_call x1, Pallas kernels: 74.4 us -> 65.2 us  [shards(): pl.pallas_call(tree_kernel, out_shape=(jax.ShapeDtypeStruct(diag_blocks.s...]
    pallas_call x1 -> x0, Pallas kernels: 4.61 us -> none  [heap_order(): pl.pallas_call(order_kernel, out_shape=jax.ShapeDtypeStruct((2 * NODES,),...]
    unnamed x5 -> x4, local copies, waits for them, and re-layouts: 3.52 us -> 2.14 us
where the time goes in v2:
time: 68.2 us; the launch traced here: 68 us
  Pallas kernels  65.2 us (96%)
  local copies, waits for them, and re-layouts  2.14 us (3%)
    pallas_call x1, Pallas kernels, shards(): pl.pallas_call(tree_kernel, out_shape=(jax.ShapeDtypeStruct(diag_blocks.s...  65.2 us
    unnamed x4, local copies, waits for them, and re-layouts  2.14 us

profile of v2, /device:TPU:1, one launch (start us, length us, event | category | flops | bytes accessed | tf_op | source)
XLA Modules:
  0.0 68.0 jit_solution(2695350899851724807)
XLA Ops:
  0.6 65.2 %tree.1 = (f32[1,128,128]{2,1,0:T(8,128)}, f32[1,1,128,128]{3,2,1,0:T(8,128)}) custom-call(s32[2,64]{1,0:T(2,128)} %bitcast.1, f32[1,128,128]{2,1,0:T(8,128)} %diag_in.1, f32[1,1,128,128]{3,2,1,0:T(8,128)} %panel_in.1), custom_call_target="tpu_custom_call" | custom-call | tf_op jit(solution)/shard_map/tree/pallas_call | solution.py:446
  65.8 0.0 copy-start
  65.8 1.5 %copy.7 = f32[1,128,128]{2,1,0:T(8,128)} copy(f32[1,128,128]{2,1,0:T(8,128)} %get-tuple-element.4) | data formatting | bytes 131072
  67.3 0.0 copy-done
  67.3 0.6 copy.8
Async XLA Ops:
  65.8 1.5 %copy-start = (f32[1,1,128,128]{3,2,1,0:T(8,128)S(1)}, f32[1,1,128,128]{3,2,1,0:T(8,128)}, u32[]{:S(2)}) copy-start(f32[1,1,128,128]{3,2,1,0:T(8,128)} %get-tuple-element.5) | copy-start | bytes 196612

commit v3 on v2

v3 whole, which is shorter than its diff:
```python
import jax
import jax.numpy as jnp
from jax import lax
from jax.experimental import pallas as pl
from jax.experimental.pallas import tpu as pltpu
from jax.sharding import PartitionSpec as P

F32, BF16 = jnp.float32, jnp.bfloat16
MESH = pl.DeviceIdType.MESH
W = 128
NODES = 64
LEVELS = 7
BLOCK = 32
NEAR_FIRST = tuple(
    tuple(sorted(range(NODES), key=lambda s: (s // 16 + s // 4 % 4 + s % 4, (s * 7 + 16 * turn) % NODES)))
    for turn in range(4)
)
PART = 16


def power_of_two(n, most):
    result = jnp.ones_like(n)
    for k in range(1, most + 1):
        result = result * jnp.where(n >= k, 2.0, 1.0)
    return result


def heap_order(parent):
    def dot(a, b, over):
        return lax.dot_general(
            a.astype(BF16), b.astype(BF16), ((over[:1], over[1:]), ((), ())), preferred_element_type=F32
        )

    down = lax.broadcasted_iota(jnp.int32, (NODES, NODES), 0)
    across = lax.broadcasted_iota(jnp.int32, (NODES, NODES), 1)
    one = (down == parent).astype(F32)
    two = dot(one, one, (1, 0))
    four = dot(two, two, (1, 0))
    alive = jnp.broadcast_to((parent < NODES).astype(F32), (8, NODES))
    len2 = alive + dot(alive, one, (1, 0))
    len4 = len2 + dot(len2, two, (1, 0))
    depth = len4 + dot(len4, four, (1, 0))
    path = (depth == LEVELS - 1).astype(F32)
    for above in (one, two, four):
        path = path + dot(path, above, (1, 1))
    siblings = dot(one, one, (0, 0))
    rank = jnp.sum(jnp.where(down < across, siblings, 0.0), axis=0, keepdims=True)
    beside = dot(path, siblings, (1, 0)) - path * alive
    code = alive * (1.0 - path) * jnp.maximum(beside, rank)
    code = code + (1.0 + alive) * dot(code, one, (1, 0))
    code = code + power_of_two(len2, 2) * dot(code, two, (1, 0))
    code = code + power_of_two(len4, 4) * dot(code, four, (1, 0))
    place = power_of_two(depth, LEVELS - 1) - 1.0 + code
    holds = (down == jnp.broadcast_to(place[:1], (NODES, NODES)).astype(jnp.int32)).astype(F32)
    label = lax.broadcasted_iota(jnp.int32, (8, NODES), 1).astype(F32)
    return dot(label, holds, (1, 1)), place


def in_three(x):
    high = x.astype(BF16)
    rest = x - high.astype(F32)
    middle = rest.astype(BF16)
    return high, middle, (rest - middle.astype(F32)).astype(BF16)


def wide(x, n):
    return jnp.concatenate([x] * n, axis=1)


def factor(work, after_block):
    tall = BLOCK // 8
    row = lax.broadcasted_iota(jnp.int32, (8, W), 0)

    def line(x, s):
        return jnp.broadcast_to(x[s : s + 1, :], (8, W))

    for b in range(W // BLOCK):
        start = b * BLOCK
        if b > 0:
            after_block(b - 1)
        x = [work[pl.ds(start + 8 * v, 8), :] for v in range(tall)]
        pivots = [None] * tall
        for part in range(0, BLOCK, PART):
            cols = {}
            for k in range(part, part + PART):
                for v in range(k // 8, tall):
                    cols[k, v] = jnp.broadcast_to(x[v][:, start + k : start + k + 1], (8, W))
            d = line(cols[part, part // 8], part % 8)
            for j in range(part, part + PART):
                v0, s = divmod(j, 8)
                r = lax.rsqrt(d)
                r2 = r * r
                pivots[v0] = d if s == 0 else jnp.where(row == s, d, pivots[v0])
                mult = {v: cols[j, v] * r2 for v in range(v0, tall)}
                below = dict(mult)
                below[v0] = jnp.where(row > s, mult[v0], 0.0)
                across = {k: line(cols[j, k // 8], k % 8) for k in range(j + 1, part + PART)}
                if j + 1 < part + PART:
                    near = across[j + 1]
                    d = line(cols[j + 1, (j + 1) // 8], (j + 1) % 8) - (near * near) * r2
                for k in range(j + 1, part + PART):
                    for v in range(k // 8, tall):
                        cols[k, v] = cols[k, v] - mult[v] * across[k]
                pivot = jnp.concatenate([line(x[v0][:, c * W : (c + 1) * W], s) for c in range(3)], axis=1)
                for v in range(v0, tall):
                    x[v] = x[v] - wide(below[v], 3) * pivot
        for v in range(tall):
            x[v] = x[v] * wide(lax.rsqrt(pivots[v]), 3)
            work[pl.ds(start + 8 * v, 8), :] = x[v]
        if start + BLOCK < W:
            high, middle, low3 = in_three(jnp.concatenate(x, axis=0))
            right = jnp.concatenate([high, middle, high, low3, middle, high], axis=0)
            left = jnp.concatenate(
                [p[:, :W] for p in (high, high, middle, high, middle, low3)], axis=0
            )
            update = jnp.dot(left.T[start + BLOCK :, :], right, preferred_element_type=F32)
            work[pl.ds(start + BLOCK, W - start - BLOCK), :] -= update


def tree_kernel(
    targets_in,
    diag_in,
    panel_in,
    out_diag,
    out_panel,
    targets,
    diag,
    panel,
    turned,
    got_diag,
    got_panel,
    ranks,
    order,
    by_label,
    by_place,
    back_place,
    back_label,
    work,
    kids,
    spare,
    spare_in,
    load,
    send1,
    recv1,
    send2,
    recv2,
    send_kids,
    recv_kids,
    send_spare,
    recv_spare,
    send3,
    recv3,
    send4,
    recv_diag,
    recv_panel,
):
    col = lax.axis_index("col")
    grp = lax.axis_index("grp")
    y, x, z = col // 16, (col // 4) % 4, col % 4
    upper_z, upper_x = z // 2, x // 2
    works = (upper_z + upper_x) == 2
    role = (
        (1 - grp) + 2 * (z % 2) + 4 * (x % 2) + 8 * (y // 2) + 16 * jnp.where(y % 3 == 0, 1, 0)
    )
    tile = (z % 2) + 2 * (x % 2) + 4 * y
    on_diag = (upper_z + upper_x) == 0
    on_panel = ((upper_z + upper_x) == 1) & (upper_x == grp)
    passes_in = on_panel | (on_diag & ((tile < 8) == (grp == 1)))
    passes_back = on_panel | on_diag
    kind = upper_x + 2 * upper_z
    lanes = pl.ds(pl.multiple_of(W * (kind % 3), W), W)

    def at(dz, dx, t):
        return (t // 4) * 16 + (2 * dx + (t // 2) % 2) * 4 + 2 * dz + t % 2

    def diag_passer(t, g):
        return (at(0, 0, t), g)

    def panel_passer(t, c):
        return (at(c, 1 - c, t), 1 - c)

    def worker(r):
        b3, b4 = (r // 8) % 2, r // 16
        wy = (1 - b4) * (1 + b3) + 3 * b4 * b3
        return (wy * 16 + (2 + (r // 4) % 2) * 4 + 2 + (r // 2) % 2, 1 - r % 2)

    def within(n):
        return jnp.minimum(jnp.maximum(n, 0), NODES - 1)

    def rows(n):
        return pl.ds(pl.multiple_of(n * 8, 8), 8)

    def copy(src, dst, send, recv, to):
        return pltpu.make_async_remote_copy(
            src_ref=src, dst_ref=dst, send_sem=send, recv_sem=recv, device_id=to, device_id_type=MESH
        )

    def repeat(n, body, group=4):
        def several(i, carry):
            for k in range(group):
                body(i * group + k)
            return carry

        lax.fori_loop(0, n // group, several, 0)

    loads = [
        pltpu.make_async_copy(src, dst, load.at[k])
        for k, (src, dst) in enumerate(((targets_in, targets), (diag_in, diag), (panel_in, panel)))
    ]
    for one in loads:
        one.start()

    barrier = pltpu.get_barrier_semaphore()

    def greet(to):
        pl.semaphore_signal(barrier, inc=1, device_id=to, device_id_type=MESH)

    @pl.when(passes_in)
    def _():
        for s in NEAR_FIRST[0]:
            greet((s, 1 - grp))

    greet((col, 1 - grp))

    @pl.when(works)
    def _():
        kids[0] = jnp.zeros((2, W, 2 * W), BF16)
        spare[0] = jnp.zeros((W, W), F32)
        spare_in[0] = jnp.zeros((W, W), F32)

    loads[0].wait()

    @pl.when(passes_back)
    def _():
        with jax.named_scope("order"):
            node, place = heap_order(targets[0:1, :])
            ranks[:, :NODES] = node.astype(jnp.int32)
            ranks[:, NODES:] = place.astype(jnp.int32)
            to_scalar = pltpu.make_async_copy(ranks, order, load.at[3])
            to_scalar.start()
            to_scalar.wait()

    loads[1].wait()
    loads[2].wait()
    turned[...] = panel[0, 0].T
    with jax.named_scope("barrier"):
        pl.semaphore_wait(barrier, 24 + 1)

    def spread_panel(i):
        t = (i + col) % 16
        copy(
            turned.at[rows(t)], by_label.at[col], send1, recv1, (at(grp, 1 - grp, t), 1 - grp)
        ).start()

    def spread_diag(i):
        t = 8 * grp + (i + col) % 8
        copy(diag.at[0, rows(t)], by_label.at[col], send1, recv1, diag_passer(t, 1 - grp)).start()

    with jax.named_scope("spread"):
        repeat(8, spread_diag)
        repeat(16, spread_panel)

    def came_back(step):
        tiles = back_place.at[pl.ds(0, 1 if step == 0 else 1 << (6 - step))]
        pltpu.make_async_copy(tiles, tiles, recv3.at[step]).wait()

    @pl.when(passes_in)
    def _():
        with jax.named_scope("wait1"):
            pltpu.make_async_copy(by_label, by_label, recv1).wait()

        def place(h):
            by_place[h] = by_label[within(order[0, h])]

        for h in range(NODES):
            place(h)

        def hand_in(step, h, r):
            copy(
                by_place.at[h], work.at[step, rows(tile), lanes], send2.at[max(step - 1, 0)], recv2.at[step], worker(r)
            ).start()

        with jax.named_scope("handin"):
            hand_in(0, NODES - 1, 0)
            for turn in range(4):

                @pl.when((tile + kind) % 4 == turn)
                def _(turn=turn):
                    for i in range(32):
                        r = (i + 8 * turn) % 32
                        hand_in(1, 31 + r, r)

            first = by_place.at[pl.ds(0, 33)]
            pltpu.make_async_copy(first, first, send2.at[0]).wait()
            for step in range(2, LEVELS):
                count = 1 << (6 - step)
                if step in (3, 4):
                    left = by_place.at[pl.ds(0, 2 * count)]
                    pltpu.make_async_copy(left, left, send2.at[step - 2]).wait()
                for r in range(count):
                    hand_in(step, count - 1 + r, r << (step - 1))

    def active(step, stride):
        return (role % stride == 0) & ((step > 0) | (role == 0))

    def climb(step, carry):
        stride, first = carry

        @pl.when(active(step, stride))
        def _():
            prev = jnp.maximum(step - 1, 0)
            gives = (role // stride) % 2 == 1
            partner = worker(jnp.maximum(role - stride, 0))
            mine = work.at[step]
            with jax.named_scope("waitheld"):
                pltpu.make_async_copy(mine, mine, recv2.at[step]).wait()

            @pl.when(step > 1)
            def _():
                with jax.named_scope("waitkids"):
                    pltpu.make_async_copy(spare_in.at[prev], spare_in.at[prev], recv_spare.at[prev]).wait()
                    for block in range(W // BLOCK):
                        lines = kids.at[prev, 1, pl.ds(BLOCK * block, BLOCK)]
                        pltpu.make_async_copy(lines, lines, recv_kids.at[prev, block]).wait()

            both = jnp.concatenate([kids[prev, 0], kids[prev, 1]], axis=0)
            update = jnp.dot(both[:, :W].T, both, preferred_element_type=F32)
            work[step, :, :W] -= update[:, :W] + (spare[prev] + spare_in[prev])
            work[step, :, W : 2 * W] -= update[:, W:]
            spare[step] = jnp.dot(both[:, W:].T, both[:, W:], preferred_element_type=F32)

            def give(block):
                lines = pl.ds(BLOCK * block, BLOCK)
                kids[step, 0, lines, :] = mine[lines, W:].astype(BF16)

                @pl.when(gives)
                def _():
                    if block == 0:
                        copy(
                            spare.at[step], spare_in.at[step], send_spare, recv_spare.at[step], partner
                        ).start()
                    copy(
                        kids.at[step, 0, lines],
                        kids.at[step, 1, lines],
                        send_kids.at[block],
                        recv_kids.at[step, block],
                        partner,
                    ).start()

            with jax.named_scope("factor"):
                factor(mine, give)
            give(W // BLOCK - 1)
            place = first + role // stride

            def hand_out(t, c, to):
                copy(
                    work.at[step, pl.ds(8 * t, 8), pl.ds(W * c, W)],
                    back_place.at[place],
                    send3.at[step],
                    recv3.at[step],
                    to,
                ).start()

            with jax.named_scope("handout"):
                for t in range(16):
                    for g in range(2):
                        hand_out(t, 0, diag_passer(t, g))
                        hand_out(t, 1 + g, panel_passer(t, g))

        return jnp.where(step == 0, 1, stride * 2), first // 2

    @pl.when(works)
    def _():
        lax.fori_loop(0, LEVELS, climb, (1, NODES - 1))

    @pl.when(passes_back)
    def _():
        with jax.named_scope("wait3"):
            for step in range(LEVELS):
                came_back(step)

        def unplace(s):
            back_label[s] = back_place[within(order[0, NODES + s])]

        for s in range(NODES):
            unplace(s)

    def hand_back(s, to, recv):
        copy(back_label.at[s], to, send4, recv, (s, 1 - grp)).start()

    for turn in range(4):

        @pl.when(on_diag & (tile % 4 == turn))
        def _(turn=turn):
            for s in NEAR_FIRST[turn]:
                hand_back(s, got_diag.at[rows(tile)], recv_diag)

        @pl.when(on_panel & (tile % 4 == turn))
        def _(turn=turn):
            for s in NEAR_FIRST[turn]:
                hand_back(s, got_panel.at[rows(tile)], recv_panel)

    with jax.named_scope("waitfinal"):
        pltpu.make_async_copy(got_diag, got_diag, recv_diag).wait()
        pltpu.make_async_copy(got_panel, got_panel, recv_panel).wait()
    down = lax.broadcasted_iota(jnp.int32, (W, W), 0)
    across = lax.broadcasted_iota(jnp.int32, (W, W), 1)
    out_diag[0] = jnp.where(across >= down, got_diag[...], 0.0).T
    out_panel[0, 0] = got_panel[...].T

    sent = by_label.at[pl.ds(0, 24)]
    pltpu.make_async_copy(sent, sent, send1).wait()

    @pl.when(passes_in)
    def _():
        for step in range(4, LEVELS):
            later = by_place.at[pl.ds(0, 1 << (6 - step))]
            pltpu.make_async_copy(later, later, send2.at[step - 1]).wait()

    @pl.when(works)
    def _():
        def drain(step, stride):
            @pl.when(active(step, stride))
            def _():
                pltpu.make_async_copy(by_label, by_label, send3.at[step]).wait()

            return jnp.where(step == 0, 1, stride * 2)

        lax.fori_loop(0, LEVELS, drain, 1)

        @pl.when(role > 0)
        def _():
            for block in range(W // BLOCK):
                lines = kids.at[0, 0, pl.ds(BLOCK * block, BLOCK)]
                pltpu.make_async_copy(lines, lines, send_kids.at[block]).wait()
            pltpu.make_async_copy(spare.at[0], spare.at[0], send_spare).wait()

    @pl.when(passes_back)
    def _():
        pltpu.make_async_copy(back_label, back_label, send4).wait()


def shards(diag_blocks, panel_blocks, targets):
    dma = pltpu.SemaphoreType.DMA
    tiles = pltpu.VMEM((NODES, 8, W), F32)
    return pl.pallas_call(
        tree_kernel,
        out_shape=(
            pltpu.VMEM(diag_blocks.shape, F32),
            pltpu.VMEM(panel_blocks.shape, F32),
        ),
        in_specs=[pl.BlockSpec(memory_space=pl.ANY)] * 3,
        out_specs=(pl.BlockSpec(memory_space=pltpu.VMEM),) * 2,
        scratch_shapes=[
            pltpu.VMEM((2, NODES), jnp.int32),
            pltpu.VMEM(diag_blocks.shape, F32),
            pltpu.VMEM(panel_blocks.shape, F32),
            pltpu.VMEM((W, W), F32),
            pltpu.VMEM((W, W), F32),
            pltpu.VMEM((W, W), F32),
            pltpu.VMEM((8, 2 * NODES), jnp.int32),
            pltpu.SMEM((8, 2 * NODES), jnp.int32),
            tiles,
            tiles,
            tiles,
            tiles,
            pltpu.VMEM((LEVELS, W, 3 * W), F32),
            pltpu.VMEM((LEVELS, 2, W, 2 * W), BF16),
            pltpu.VMEM((LEVELS, W, W), F32),
            pltpu.VMEM((LEVELS, W, W), F32),
            dma((4,)),
            dma,
            dma,
            dma((LEVELS - 1,)),
            dma((LEVELS,)),
            dma((W // BLOCK,)),
            dma((LEVELS, W // BLOCK)),
            dma,
            dma((LEVELS,)),
            dma((LEVELS,)),
            dma((LEVELS,)),
            dma,
            dma,
            dma,
        ],
        compiler_params=pltpu.CompilerParams(collective_id=0, has_side_effects=True),
        name="tree",
    )(targets.T, diag_blocks, panel_blocks)


def solution(mesh):
    placed = (P("col", None, None), P("col", "grp", None, None), P())
    return jax.shard_map(
        shards,
        mesh=mesh,
        in_specs=placed,
        out_specs=(P("col", None, None), P("col", "grp", None, None)),
        check_vma=False,
    )
```

time: 68.2 us -> 62.5 us (0.916)
  Pallas kernels: 65.2 us -> 60.5 us
  local copies, waits for them, and re-layouts: 2.14 us -> 1.26 us
    pallas_call x1, Pallas kernels: 65.2 us -> 60.5 us  [shards(): pl.pallas_call(tree_kernel, out_shape=(pltpu.VMEM(diag_blocks.shape, F32)...]
    unnamed x4 -> x2, local copies, waits for them, and re-layouts: 2.14 us -> 1.26 us
where the time goes in v3:
time: 62.5 us; the launch traced here: 62.4 us
  Pallas kernels  60.5 us (97%)
  local copies, waits for them, and re-layouts  1.26 us (2%)
  between operations  0.64 us (1%)
    pallas_call x1, Pallas kernels, shards(): pl.pallas_call(tree_kernel, out_shape=(pltpu.VMEM(diag_blocks.shape, F32)...  60.5 us
    unnamed x2, local copies, waits for them, and re-layouts  1.26 us

profile of v3, /device:TPU:1, one launch (start us, length us, event | category | flops | bytes accessed | tf_op | source)
XLA Modules:
  0.0 62.4 jit_solution(13675083177463567322)
XLA Ops:
  0.6 60.5 %tree.1 = (f32[1,128,128]{2,1,0:T(8,128)S(1)}, f32[1,1,128,128]{3,2,1,0:T(8,128)S(1)}) custom-call(s32[2,64]{1,0:T(2,128)} %bitcast.1, f32[1,128,128]{2,1,0:T(8,128)} %diag_in.1, f32[1,1,128,128]{3,2,1,0:T(8,128)} %panel_in.1), custom_call_target="tpu_custom_call" | custom-call | tf_op jit(solution)/shard_map/tree/pallas_call | solution.py:446
  61.1 0.6 %copy.7 = f32[1,128,128]{2,1,0:T(8,128)} copy(f32[1,128,128]{2,1,0:T(8,128)S(1)} %get-tuple-element.2) | data formatting | bytes 131072
  61.7 0.6 %copy.8 = f32[1,1,128,128]{3,2,1,0:T(8,128)} copy(f32[1,1,128,128]{3,2,1,0:T(8,128)S(1)} %get-tuple-element.3) | data formatting | bytes 131072

commit v4 on v3

--- a/solution.py
+++ b/solution.py
@@ -83,8 +83,9 @@
         for part in range(0, BLOCK, PART):
             cols = {}
             for k in range(part, part + PART):
+                lane = jnp.full((8, W), start + k, jnp.int32)
                 for v in range(k // 8, tall):
-                    cols[k, v] = jnp.broadcast_to(x[v][:, start + k : start + k + 1], (8, W))
+                    cols[k, v] = jnp.take_along_axis(x[v][:, :W], lane, axis=1)
             d = line(cols[part, part // 8], part % 8)
             for j in range(part, part + PART):
                 v0, s = divmod(j, 8)
@@ -162,16 +163,16 @@
     role = (
         (1 - grp) + 2 * (z % 2) + 4 * (x % 2) + 8 * (y // 2) + 16 * jnp.where(y % 3 == 0, 1, 0)
     )
-    tile = (z % 2) + 2 * (x % 2) + 4 * y
+    tile = (z % 2) + 2 * (x % 2) + 4 * ((y + 2) % 4)
     on_diag = (upper_z + upper_x) == 0
     on_panel = ((upper_z + upper_x) == 1) & (upper_x == grp)
     passes_in = on_panel | (on_diag & ((tile < 8) == (grp == 1)))
     passes_back = on_panel | on_diag
-    kind = upper_x + 2 * upper_z
-    lanes = pl.ds(pl.multiple_of(W * (kind % 3), W), W)
+    kind = jnp.where(on_panel, 2 - grp, 0)
+    lanes = pl.ds(pl.multiple_of(W * kind, W), W)
 
     def at(dz, dx, t):
-        return (t // 4) * 16 + (2 * dx + (t // 2) % 2) * 4 + 2 * dz + t % 2
+        return ((t // 4 + 2) % 4) * 16 + (2 * dx + (t // 2) % 2) * 4 + 2 * dz + t % 2
 
     def diag_passer(t, g):
         return (at(0, 0, t), g)
@@ -227,6 +228,24 @@
         kids[0] = jnp.zeros((2, W, 2 * W), BF16)
         spare[0] = jnp.zeros((W, W), F32)
         spare_in[0] = jnp.zeros((W, W), F32)
+
+    loads[1].wait()
+    loads[2].wait()
+    turned[...] = panel[0, 0].T
+    with jax.named_scope("barrier"):
+        pl.semaphore_wait(barrier, 24 + 1)
+
+    def spread_panel(i):
+        t = (i + col) % 16
+        copy(turned.at[rows(t)], by_label.at[col], send1, recv1, (at(grp, 1 - grp, t), 1 - grp)).start()
+
+    def spread_diag(i):
+        t = 8 * grp + (i + col) % 8
+        copy(diag.at[0, rows(t)], by_label.at[col], send1, recv1, diag_passer(t, 1 - grp)).start()
+
+    with jax.named_scope("spread"):
+        repeat(8, spread_diag)
+        repeat(16, spread_panel)
 
     loads[0].wait()
 
@@ -239,26 +258,6 @@
             to_scalar = pltpu.make_async_copy(ranks, order, load.at[3])
             to_scalar.start()
             to_scalar.wait()
-
-    loads[1].wait()
-    loads[2].wait()
-    turned[...] = panel[0, 0].T
-    with jax.named_scope("barrier"):
-        pl.semaphore_wait(barrier, 24 + 1)
-
-    def spread_panel(i):
-        t = (i + col) % 16
-        copy(
-            turned.at[rows(t)], by_label.at[col], send1, recv1, (at(grp, 1 - grp, t), 1 - grp)
-        ).start()
-
-    def spread_diag(i):
-        t = 8 * grp + (i + col) % 8
-        copy(diag.at[0, rows(t)], by_label.at[col], send1, recv1, diag_passer(t, 1 - grp)).start()
-
-    with jax.named_scope("spread"):
-        repeat(8, spread_diag)
-        repeat(16, spread_panel)
 
     def came_back(step):
         tiles = back_place.at[pl.ds(0, 1 if step == 0 else 1 << (6 - step))]
@@ -311,6 +310,7 @@
             prev = jnp.maximum(step - 1, 0)
             gives = (role // stride) % 2 == 1
             partner = worker(jnp.maximum(role - stride, 0))
+            place = first + role // stride
             mine = work.at[step]
             with jax.named_scope("waitheld"):
                 pltpu.make_async_copy(mine, mine, recv2.at[step]).wait()
@@ -328,6 +328,15 @@
             work[step, :, :W] -= update[:, :W] + (spare[prev] + spare_in[prev])
             work[step, :, W : 2 * W] -= update[:, W:]
             spare[step] = jnp.dot(both[:, W:].T, both[:, W:], preferred_element_type=F32)
+
+            def hand_out(t, c, to):
+                copy(
+                    work.at[step, pl.ds(8 * t, 8), pl.ds(W * c, W)],
+                    back_place.at[place],
+                    send3.at[step],
+                    recv3.at[step],
+                    to,
+                ).start()
 
             def give(block):
                 lines = pl.ds(BLOCK * block, BLOCK)
@@ -347,25 +356,25 @@
                         partner,
                     ).start()
 
+                def hand_out_rows(first, count):
+                    for t in range(first, first + count):
+                        for g in range(2):
+                            hand_out(t, 0, diag_passer(t, g))
+                            hand_out(t, 1 + g, panel_passer(t, g))
+
+                @pl.when(step == LEVELS - 1)
+                def _():
+                    hand_out_rows(4 * block, 4)
+
+                if block == W // BLOCK - 1:
+
+                    @pl.when(step < LEVELS - 1)
+                    def _():
+                        hand_out_rows(0, 16)
+
             with jax.named_scope("factor"):
                 factor(mine, give)
             give(W // BLOCK - 1)
-            place = first + role // stride
-
-            def hand_out(t, c, to):
-                copy(
-                    work.at[step, pl.ds(8 * t, 8), pl.ds(W * c, W)],
-                    back_place.at[place],
-                    send3.at[step],
-                    recv3.at[step],
-                    to,
-                ).start()
-
-            with jax.named_scope("handout"):
-                for t in range(16):
-                    for g in range(2):
-                        hand_out(t, 0, diag_passer(t, g))
-                        hand_out(t, 1 + g, panel_passer(t, g))
 
         return jnp.where(step == 0, 1, stride * 2), first // 2
 
@@ -399,6 +408,37 @@
         def _(turn=turn):
             for s in NEAR_FIRST[turn]:
                 hand_back(s, got_panel.at[rows(tile)], recv_panel)
+
+    sent = by_label.at[pl.ds(0, 24)]
+    pltpu.make_async_copy(sent, sent, send1).wait()
+
+    @pl.when(passes_in)
+    def _():
+        for step in range(4, LEVELS):
+            later = by_place.at[pl.ds(0, 1 << (6 - step))]
+            pltpu.make_async_copy(later, later, send2.at[step - 1]).wait()
+
+    @pl.when(works)
+    def _():
+        def drain(step, stride):
+            @pl.when(active(step, stride))
+            def _():
+                pltpu.make_async_copy(by_label, by_label, send3.at[step]).wait()
+
+            return jnp.where(step == 0, 1, stride * 2)
+
+        lax.fori_loop(0, LEVELS, drain, 1)
+
+        @pl.when(role > 0)
+        def _():
+            for block in range(W // BLOCK):
+                lines = kids.at[0, 0, pl.ds(BLOCK * block, BLOCK)]
+                pltpu.make_async_copy(lines, lines, send_kids.at[block]).wait()
+            pltpu.make_async_copy(spare.at[0], spare.at[0], send_spare).wait()
+
+    @pl.when(passes_back)
+    def _():
+        pltpu.make_async_copy(back_label, back_label, send4).wait()
 
     with jax.named_scope("waitfinal"):
         pltpu.make_async_copy(got_diag, got_diag, recv_diag).wait()
@@ -407,37 +447,6 @@
     across = lax.broadcasted_iota(jnp.int32, (W, W), 1)
     out_diag[0] = jnp.where(across >= down, got_diag[...], 0.0).T
     out_panel[0, 0] = got_panel[...].T
-
-    sent = by_label.at[pl.ds(0, 24)]
-    pltpu.make_async_copy(sent, sent, send1).wait()
-
-    @pl.when(passes_in)
-    def _():
-        for step in range(4, LEVELS):
-            later = by_place.at[pl.ds(0, 1 << (6 - step))]
-            pltpu.make_async_copy(later, later, send2.at[step - 1]).wait()
-
-    @pl.when(works)
-    def _():
-        def drain(step, stride):
-            @pl.when(active(step, stride))
-            def _():
-                pltpu.make_async_copy(by_label, by_label, send3.at[step]).wait()
-
-            return jnp.where(step == 0, 1, stride * 2)
-
-        lax.fori_loop(0, LEVELS, drain, 1)
-
-        @pl.when(role > 0)
-        def _():
-            for block in range(W // BLOCK):
-                lines = kids.at[0, 0, pl.ds(BLOCK * block, BLOCK)]
-                pltpu.make_async_copy(lines, lines, send_kids.at[block]).wait()
-            pltpu.make_async_copy(spare.at[0], spare.at[0], send_spare).wait()
-
-    @pl.when(passes_back)
-    def _():
-        pltpu.make_async_copy(back_label, back_label, send4).wait()
 
 
 def shards(diag_blocks, panel_blocks, targets):

time: 62.5 us -> 58.4 us (0.934)
  Pallas kernels: 60.5 us -> 56.3 us
    pallas_call x1, Pallas kernels: 60.5 us -> 56.3 us  [shards(): pl.pallas_call(tree_kernel, out_shape=(pltpu.VMEM(diag_blocks.shape, F32)...]
where the time goes in v4:
time: 58.4 us; the launch traced here: 58.2 us
  Pallas kernels  56.3 us (96%)
  local copies, waits for them, and re-layouts  1.26 us (2%)
  between operations  0.64 us (1%)
    pallas_call x1, Pallas kernels, shards(): pl.pallas_call(tree_kernel, out_shape=(pltpu.VMEM(diag_blocks.shape, F32)...  56.3 us
    unnamed x2, local copies, waits for them, and re-layouts  1.26 us

profile of v4, /device:TPU:1, one launch (start us, length us, event | category | flops | bytes accessed | tf_op | source)
XLA Modules:
  0.0 58.2 jit_solution(98777770517602526)
XLA Ops:
  0.6 56.3 %tree.1 = (f32[1,128,128]{2,1,0:T(8,128)S(1)}, f32[1,1,128,128]{3,2,1,0:T(8,128)S(1)}) custom-call(s32[2,64]{1,0:T(2,128)} %bitcast.1, f32[1,128,128]{2,1,0:T(8,128)} %diag_in.1, f32[1,1,128,128]{3,2,1,0:T(8,128)} %panel_in.1), custom_call_target="tpu_custom_call" | custom-call | tf_op jit(solution)/shard_map/tree/pallas_call | solution.py:455
  57.0 0.6 %copy.7 = f32[1,128,128]{2,1,0:T(8,128)} copy(f32[1,128,128]{2,1,0:T(8,128)S(1)} %get-tuple-element.2) | data formatting | bytes 131072
  57.6 0.6 %copy.8 = f32[1,1,128,128]{3,2,1,0:T(8,128)} copy(f32[1,1,128,128]{3,2,1,0:T(8,128)S(1)} %get-tuple-element.3) | data formatting | bytes 131072

commit v5 on v4

--- a/solution.py
+++ b/solution.py
@@ -161,7 +161,7 @@
     upper_z, upper_x = z // 2, x // 2
     works = (upper_z + upper_x) == 2
     role = (
-        (1 - grp) + 2 * (z % 2) + 4 * (x % 2) + 8 * (y // 2) + 16 * jnp.where(y % 3 == 0, 1, 0)
+        (1 - grp) + 2 * (z % 2) + 4 * (x % 2) + 8 * jnp.where(y % 3 == 0, 1, 0) + 16 * (y // 2)
     )
     tile = (z % 2) + 2 * (x % 2) + 4 * ((y + 2) % 4)
     on_diag = (upper_z + upper_x) == 0
@@ -182,7 +182,7 @@
 
     def worker(r):
         b3, b4 = (r // 8) % 2, r // 16
-        wy = (1 - b4) * (1 + b3) + 3 * b4 * b3
+        wy = (1 - b4) * (1 - b3) + b4 * (2 + b3)
         return (wy * 16 + (2 + (r // 4) % 2) * 4 + 2 + (r // 2) % 2, 1 - r % 2)
 
     def within(n):
@@ -449,10 +449,21 @@
     out_panel[0, 0] = got_panel[...].T
 
 
+def deliver_kernel(diag, panel, out_diag, out_panel, sems):
+    copies = [
+        pltpu.make_async_copy(diag, out_diag, sems.at[0]),
+        pltpu.make_async_copy(panel, out_panel, sems.at[1]),
+    ]
+    for one in copies:
+        one.start()
+    for one in copies:
+        one.wait()
+
+
 def shards(diag_blocks, panel_blocks, targets):
     dma = pltpu.SemaphoreType.DMA
     tiles = pltpu.VMEM((NODES, 8, W), F32)
-    return pl.pallas_call(
+    factors = pl.pallas_call(
         tree_kernel,
         out_shape=(
             pltpu.VMEM(diag_blocks.shape, F32),
@@ -495,6 +506,14 @@
         compiler_params=pltpu.CompilerParams(collective_id=0, has_side_effects=True),
         name="tree",
     )(targets.T, diag_blocks, panel_blocks)
+    return pl.pallas_call(
+        deliver_kernel,
+        out_shape=tuple(jax.ShapeDtypeStruct(f.shape, F32) for f in factors),
+        in_specs=(pl.BlockSpec(memory_space=pltpu.VMEM),) * 2,
+        out_specs=(pl.BlockSpec(memory_space=pl.ANY),) * 2,
+        scratch_shapes=[dma((2,))],
+        name="deliver",
+    )(*(pltpu.with_memory_space_constraint(f, pltpu.VMEM) for f in factors))
 
 
 def solution(mesh):

time: 58.4 us -> 57.2 us (0.979)
  local copies, waits for them, and re-layouts: 1.26 us -> 0 us
    unnamed x2 -> x0, local copies, waits for them, and re-layouts: 1.26 us -> none
    pallas_call x0 -> x1, Pallas kernels: none -> 0.67 us  [shards(): pl.pallas_call(deliver_kernel, out_shape=tuple((jax.ShapeDtypeStruct(f.sh...]
    pallas_call x1, Pallas kernels: 56.3 us -> 55.8 us  [shards(): pl.pallas_call(tree_kernel, out_shape=(pltpu.VMEM(diag_blocks.shape, F32)...]
where the time goes in v5:
time: 57.2 us; the launch traced here: 57.1 us
  Pallas kernels  56.4 us (99%)
  between operations  0.64 us (1%)
    pallas_call x1, Pallas kernels, shards(): pl.pallas_call(tree_kernel, out_shape=(pltpu.VMEM(diag_blocks.shape, F32)...  55.8 us

profile of v5, /device:TPU:1, one launch (start us, length us, event | category | flops | bytes accessed | tf_op | source)
XLA Modules:
  0.0 57.1 jit_solution(2227349460630943953)
XLA Ops:
  0.6 55.8 %tree.1 = (f32[1,128,128]{2,1,0:T(8,128)S(1)}, f32[1,1,128,128]{3,2,1,0:T(8,128)S(1)}) custom-call(s32[2,64]{1,0:T(2,128)} %bitcast.1, f32[1,128,128]{2,1,0:T(8,128)} %diag_in.1, f32[1,1,128,128]{3,2,1,0:T(8,128)} %panel_in.1), custom_call_target="tpu_custom_call" | custom-call | tf_op jit(solution)/shard_map/tree/pallas_call | solution.py:466
  56.4 0.7 %deliver.1 = (f32[1,128,128]{2,1,0:T(8,128)}, f32[1,1,128,128]{3,2,1,0:T(8,128)}) custom-call(f32[1,128,128]{2,1,0:T(8,128)S(1)} %get-tuple-element.4.diag, f32[1,1,128,128]{3,2,1,0:T(8,128)S(1)} %get-tuple-element.5.panel), custom_call_target="tpu_custom_call" | custom-call | tf_op jit(solution)/shard_map/deliver/pallas_call | solution.py:509

commit v6 on v5

--- a/solution.py
+++ b/solution.py
@@ -259,10 +259,6 @@
             to_scalar.start()
             to_scalar.wait()
 
-    def came_back(step):
-        tiles = back_place.at[pl.ds(0, 1 if step == 0 else 1 << (6 - step))]
-        pltpu.make_async_copy(tiles, tiles, recv3.at[step]).wait()
-
     @pl.when(passes_in)
     def _():
         with jax.named_scope("wait1"):
@@ -276,7 +272,7 @@
 
         def hand_in(step, h, r):
             copy(
-                by_place.at[h], work.at[step, rows(tile), lanes], send2.at[max(step - 1, 0)], recv2.at[step], worker(r)
+                by_place.at[h], work.at[step, rows(tile), lanes], send2.at[min(max(step - 1, 0), 3)], recv2.at[step], worker(r)
             ).start()
 
         with jax.named_scope("handin"):
@@ -310,6 +306,7 @@
             prev = jnp.maximum(step - 1, 0)
             gives = (role // stride) % 2 == 1
             partner = worker(jnp.maximum(role - stride, 0))
+            given = jnp.maximum(step - 1, 0)
             place = first + role // stride
             mine = work.at[step]
             with jax.named_scope("waitheld"):
@@ -318,10 +315,8 @@
             @pl.when(step > 1)
             def _():
                 with jax.named_scope("waitkids"):
-                    pltpu.make_async_copy(spare_in.at[prev], spare_in.at[prev], recv_spare.at[prev]).wait()
-                    for block in range(W // BLOCK):
-                        lines = kids.at[prev, 1, pl.ds(BLOCK * block, BLOCK)]
-                        pltpu.make_async_copy(lines, lines, recv_kids.at[prev, block]).wait()
+                    pltpu.make_async_copy(spare_in.at[prev], spare_in.at[prev], recv_spare.at[prev - 1]).wait()
+                    pltpu.make_async_copy(kids.at[prev, 1], kids.at[prev, 1], recv_kids.at[prev - 1]).wait()
 
             both = jnp.concatenate([kids[prev, 0], kids[prev, 1]], axis=0)
             update = jnp.dot(both[:, :W].T, both, preferred_element_type=F32)
@@ -334,7 +329,7 @@
                     work.at[step, pl.ds(8 * t, 8), pl.ds(W * c, W)],
                     back_place.at[place],
                     send3.at[step],
-                    recv3.at[step],
+                    recv3,
                     to,
                 ).start()
 
@@ -346,13 +341,13 @@
                 def _():
                     if block == 0:
                         copy(
-                            spare.at[step], spare_in.at[step], send_spare, recv_spare.at[step], partner
+                            spare.at[step], spare_in.at[step], send_spare, recv_spare.at[given], partner
                         ).start()
                     copy(
                         kids.at[step, 0, lines],
                         kids.at[step, 1, lines],
-                        send_kids.at[block],
-                        recv_kids.at[step, block],
+                        send_kids,
+                        recv_kids.at[given],
                         partner,
                     ).start()
 
@@ -385,8 +380,7 @@
     @pl.when(passes_back)
     def _():
         with jax.named_scope("wait3"):
-            for step in range(LEVELS):
-                came_back(step)
+            pltpu.make_async_copy(back_place, back_place, recv3).wait()
 
         def unplace(s):
             back_label[s] = back_place[within(order[0, NODES + s])]
@@ -414,9 +408,8 @@
 
     @pl.when(passes_in)
     def _():
-        for step in range(4, LEVELS):
-            later = by_place.at[pl.ds(0, 1 << (6 - step))]
-            pltpu.make_async_copy(later, later, send2.at[step - 1]).wait()
+        later = by_place.at[pl.ds(0, 7)]
+        pltpu.make_async_copy(later, later, send2.at[3]).wait()
 
     @pl.when(works)
     def _():
@@ -431,9 +424,7 @@
 
         @pl.when(role > 0)
         def _():
-            for block in range(W // BLOCK):
-                lines = kids.at[0, 0, pl.ds(BLOCK * block, BLOCK)]
-                pltpu.make_async_copy(lines, lines, send_kids.at[block]).wait()
+            pltpu.make_async_copy(kids.at[0, 0], kids.at[0, 0], send_kids).wait()
             pltpu.make_async_copy(spare.at[0], spare.at[0], send_spare).wait()
 
     @pl.when(passes_back)
@@ -491,14 +482,14 @@
             dma((4,)),
             dma,
             dma,
-            dma((LEVELS - 1,)),
+            dma((4,)),
             dma((LEVELS,)),
-            dma((W // BLOCK,)),
-            dma((LEVELS, W // BLOCK)),
-            dma,
+            dma,
+            dma((LEVELS - 2,)),
+            dma,
+            dma((LEVELS - 2,)),
             dma((LEVELS,)),
-            dma((LEVELS,)),
-            dma((LEVELS,)),
+            dma,
             dma,
             dma,
             dma,

time: 57.2 us -> 56.9 us (level)
  no operation moved by 1% of the time
where the time goes in v6:
time: 56.9 us; the launch traced here: 56.7 us
  Pallas kernels  56.1 us (99%)
  between operations  0.64 us (1%)
    pallas_call x1, Pallas kernels, shards(): pl.pallas_call(tree_kernel, out_shape=(pltpu.VMEM(diag_blocks.shape, F32)...  55.4 us

profile of v6, /device:TPU:1, one launch (start us, length us, event | category | flops | bytes accessed | tf_op | source)
XLA Modules:
  0.0 56.7 jit_solution(4219111334681100321)
XLA Ops:
  0.6 55.4 %tree.1 = (f32[1,128,128]{2,1,0:T(8,128)S(1)}, f32[1,1,128,128]{3,2,1,0:T(8,128)S(1)}) custom-call(s32[2,64]{1,0:T(2,128)} %bitcast.1, f32[1,128,128]{2,1,0:T(8,128)} %diag_in.1, f32[1,1,128,128]{3,2,1,0:T(8,128)} %panel_in.1), custom_call_target="tpu_custom_call" | custom-call | tf_op jit(solution)/shard_map/tree/pallas_call | solution.py:457
  56.1 0.7 %deliver.1 = (f32[1,128,128]{2,1,0:T(8,128)}, f32[1,1,128,128]{3,2,1,0:T(8,128)}) custom-call(f32[1,128,128]{2,1,0:T(8,128)S(1)} %get-tuple-element.4.diag, f32[1,1,128,128]{3,2,1,0:T(8,128)S(1)} %get-tuple-element.5.panel), custom_call_target="tpu_custom_call" | custom-call | tf_op jit(solution)/shard_map/deliver/pallas_call | solution.py:500

commit v7 on v6

--- a/solution.py
+++ b/solution.py
@@ -122,14 +122,12 @@
     targets_in,
     diag_in,
     panel_in,
-    out_diag,
-    out_panel,
+    got_diag,
+    got_panel,
     targets,
     diag,
     panel,
     turned,
-    got_diag,
-    got_panel,
     ranks,
     order,
     by_label,
@@ -396,12 +394,12 @@
         @pl.when(on_diag & (tile % 4 == turn))
         def _(turn=turn):
             for s in NEAR_FIRST[turn]:
-                hand_back(s, got_diag.at[rows(tile)], recv_diag)
+                hand_back(s, got_diag.at[0, rows(tile)], recv_diag)
 
         @pl.when(on_panel & (tile % 4 == turn))
         def _(turn=turn):
             for s in NEAR_FIRST[turn]:
-                hand_back(s, got_panel.at[rows(tile)], recv_panel)
+                hand_back(s, got_panel.at[0, 0, rows(tile)], recv_panel)
 
     sent = by_label.at[pl.ds(0, 24)]
     pltpu.make_async_copy(sent, sent, send1).wait()
@@ -434,19 +432,19 @@
     with jax.named_scope("waitfinal"):
         pltpu.make_async_copy(got_diag, got_diag, recv_diag).wait()
         pltpu.make_async_copy(got_panel, got_panel, recv_panel).wait()
+
+
+def deliver_kernel(diag, panel, out_diag, out_panel, turned, sems):
     down = lax.broadcasted_iota(jnp.int32, (W, W), 0)
     across = lax.broadcasted_iota(jnp.int32, (W, W), 1)
-    out_diag[0] = jnp.where(across >= down, got_diag[...], 0.0).T
-    out_panel[0, 0] = got_panel[...].T
-
-
-def deliver_kernel(diag, panel, out_diag, out_panel, sems):
     copies = [
-        pltpu.make_async_copy(diag, out_diag, sems.at[0]),
-        pltpu.make_async_copy(panel, out_panel, sems.at[1]),
+        pltpu.make_async_copy(turned.at[0], out_diag.at[0], sems.at[0]),
+        pltpu.make_async_copy(turned.at[1], out_panel.at[0, 0], sems.at[1]),
     ]
-    for one in copies:
-        one.start()
+    turned[0] = jnp.where(across >= down, diag[0], 0.0).T
+    copies[0].start()
+    turned[1] = panel[0, 0].T
+    copies[1].start()
     for one in copies:
         one.wait()
 
@@ -467,8 +465,6 @@
             pltpu.VMEM(diag_blocks.shape, F32),
             pltpu.VMEM(panel_blocks.shape, F32),
             pltpu.VMEM((W, W), F32),
-            pltpu.VMEM((W, W), F32),
-            pltpu.VMEM((W, W), F32),
             pltpu.VMEM((8, 2 * NODES), jnp.int32),
             pltpu.SMEM((8, 2 * NODES), jnp.int32),
             tiles,
@@ -502,7 +498,7 @@
         out_shape=tuple(jax.ShapeDtypeStruct(f.shape, F32) for f in factors),
         in_specs=(pl.BlockSpec(memory_space=pltpu.VMEM),) * 2,
         out_specs=(pl.BlockSpec(memory_space=pl.ANY),) * 2,
-        scratch_shapes=[dma((2,))],
+        scratch_shapes=[pltpu.VMEM((2, W, W), F32), dma((2,))],
         name="deliver",
     )(*(pltpu.with_memory_space_constraint(f, pltpu.VMEM) for f in factors))
 

time: 56.9 us -> 56.9 us (level)
  no operation moved by 1% of the time
where the time goes in v7:
time: 56.9 us; the launch traced here: 56.7 us
  Pallas kernels  56.1 us (99%)
  between operations  0.64 us (1%)
    pallas_call x1, Pallas kernels, shards(): pl.pallas_call(tree_kernel, out_shape=(pltpu.VMEM(diag_blocks.shape, F32)...  55.3 us

profile of v7, /device:TPU:1, one launch (start us, length us, event | category | flops | bytes accessed | tf_op | source)
XLA Modules:
  0.0 56.7 jit_solution(10583080249774421353)
XLA Ops:
  0.6 55.3 %tree.1 = (f32[1,128,128]{2,1,0:T(8,128)S(1)}, f32[1,1,128,128]{3,2,1,0:T(8,128)S(1)}) custom-call(s32[2,64]{1,0:T(2,128)} %bitcast.1, f32[1,128,128]{2,1,0:T(8,128)} %diag_in.1, f32[1,1,128,128]{3,2,1,0:T(8,128)} %panel_in.1), custom_call_target="tpu_custom_call" | custom-call | tf_op jit(solution)/shard_map/tree/pallas_call | solution.py:455
  56.0 0.8 %deliver.1 = (f32[1,128,128]{2,1,0:T(8,128)}, f32[1,1,128,128]{3,2,1,0:T(8,128)}) custom-call(f32[1,128,128]{2,1,0:T(8,128)S(1)} %get-tuple-element.4.diag, f32[1,1,128,128]{3,2,1,0:T(8,128)S(1)} %get-tuple-element.5.panel), custom_call_target="tpu_custom_call" | custom-call | tf_op jit(solution)/shard_map/deliver/pallas_call | solution.py:496
